TPU v7x, 128 devices: a whole 4x4x4 slice. The times are simulated.
128 devices in a mesh: node: 32 (over x_hi, z, y), shard: 4 (over x_lo, core).
Axes of the slice: x: 4 (x_hi: 2, x_lo: 2; x = x_hi * 2 + x_lo), y: 4, z: 4, core: 2. Of those that a mesh axis runs over, the one named last changes fastest.
Arguments:
- inputs: bfloat16 [32, 1024, 1152], P('node', 'shard'), may hold values from -6 to 6
- upstream: bfloat16 [32, 1024, 1152], P('node', 'shard'), may hold values from -6 to 6
- counts: int32 [32], P('node'), may hold values from 1 to 4
- round_index: int32 [1], replicated, may hold values from 0 to 999
- rates: float32 [32], P('node'), may hold values from 0.002 to 0.008
- gate_weight: bfloat16 [32, 1152, 4608], P('node', None, 'shard'), may hold values from -0.1875 to 0.1875
- up_weight: bfloat16 [32, 1152, 4608], P('node', None, 'shard'), may hold values from -0.1875 to 0.1875
- down_weight: bfloat16 [32, 4608, 1152], P('node', 'shard'), may hold values from -0.09375 to 0.09375
Outputs:
- gate_mixed: bfloat16 [32, 1152, 4608], P('node', None, 'shard')
- up_mixed: bfloat16 [32, 1152, 4608], P('node', None, 'shard')
- down_mixed: bfloat16 [32, 4608, 1152], P('node', 'shard')
Inputs may be any that keep to these rules, and one draw needn't show every extreme that they name: A node's live sequences fill its first counts slots of 4.
All inputs are finite; a program needn't handle non-finite values.
Results may differ from a plain program's by a relative error of at most 0.007.
Values may be sent and summed in bfloat16 or wider, within the bound.
A program may use at most 128 MiB of HBM per device.

v0:
```python
import jax
import jax.numpy as jnp
from jax import lax
from jax.sharding import PartitionSpec as P

SLOTS = 4


def for_sending(array):

    def short(part):
        return part.astype(jnp.bfloat16) if part.dtype == jnp.float32 else part

    return jax.tree.map(short, array)


def partner(array, axis, distance):
    return lax.ppermute(array, axis, [(i, i ^ 1 << distance) for i in range(lax.axis_size(axis))])


def sent_together(arrays, axis, dim, along):
    both = jnp.concatenate(arrays, axis=along)
    result, at, finished = (lax.all_gather(both, axis, axis=dim, tiled=True), 0, [])
    for a in arrays:
        finished.append(lax.slice_in_dim(result, at, at + a.shape[along], axis=along))
        at += a.shape[along]
    return tuple(finished)


def gelu_tanh(values):
    return jax.nn.gelu(values, approximate=True)


def slot_grads(rows, grad_out, w_gate, w_up, w_down):
    floats = rows.astype(jnp.float32)
    normed = (floats * lax.rsqrt(jnp.mean(floats * floats, -1, keepdims=True) + 1e-06)).astype(
        jnp.bfloat16
    )
    pre_gate = jnp.dot(normed, w_gate, preferred_element_type=jnp.float32)
    pre_up = jnp.dot(normed, w_up, preferred_element_type=jnp.float32)
    act, pull = jax.vjp(gelu_tanh, pre_gate)
    slope = pull(jnp.ones_like(pre_gate))[0]
    hidden = (act * pre_up).astype(jnp.bfloat16)
    back = lax.dot_general(
        grad_out, w_down, (((1,), (1,)), ((), ())), preferred_element_type=jnp.float32
    )
    d_gate = (back * pre_up * slope).astype(jnp.bfloat16)
    d_up = (back * act).astype(jnp.bfloat16)
    inner = (((0,), (0,)), ((), ()))
    grad_gate = lax.dot_general(normed, d_gate, inner, preferred_element_type=jnp.float32)
    grad_up = lax.dot_general(normed, d_up, inner, preferred_element_type=jnp.float32)
    grad_down = lax.dot_general(hidden, grad_out, inner, preferred_element_type=jnp.float32)
    return (grad_gate, grad_up, grad_down)


def pair_swap(level):

    def run(slab):
        return jax.tree.map(
            lambda part, own: part.astype(own.dtype),
            partner(for_sending(slab), "node", level),
            slab,
        )

    return run


def per_device(inputs, upstream, counts, round_index, rates, gate_weight, up_weight, down_weight):
    rows_all, grads_all = sent_together((inputs, upstream), "shard", 1, 0)
    rows_all = rows_all[0]
    grads_all = grads_all[0]
    w_gate = gate_weight[0]
    w_up = up_weight[0]
    w_down = down_weight[0]
    count = counts[0]
    seq_len = rows_all.shape[0] // SLOTS
    row_slot = lax.broadcasted_iota(jnp.int32, (rows_all.shape[0], 1), 0) // seq_len
    grad_out = jnp.where(row_slot < count, grads_all, jnp.zeros_like(grads_all))
    grad_gate, grad_up, grad_down = slot_grads(rows_all, grad_out, w_gate, w_up, w_down)
    decay = 250.0 / (250.0 + round_index[0].astype(jnp.float32))
    step_size = rates[0] * decay
    new_gate = (w_gate.astype(jnp.float32) - step_size * grad_gate).astype(jnp.bfloat16)
    new_up = (w_up.astype(jnp.float32) - step_size * grad_up).astype(jnp.bfloat16)
    new_down = (w_down.astype(jnp.float32) - step_size * grad_down).astype(jnp.bfloat16)
    slab = (new_gate, new_up, new_down)
    levels = lax.axis_size("node").bit_length() - 1
    which = round_index[0] % levels
    branches = [pair_swap(level) for level in range(levels)]
    received = lax.switch(which, branches, slab)
    mixed = [
        (0.5 * (mine.astype(jnp.float32) + theirs.astype(jnp.float32))).astype(jnp.bfloat16)
        for mine, theirs in zip(slab, received)
    ]
    return (mixed[0][None], mixed[1][None], mixed[2][None])


def solution(mesh):
    return jax.shard_map(
        per_device,
        mesh=mesh,
        in_specs=(
            P("node", "shard", None),
            P("node", "shard", None),
            P("node"),
            P(),
            P("node"),
            P("node", None, "shard"),
            P("node", None, "shard"),
            P("node", "shard", None),
        ),
        out_specs=(P("node", None, "shard"), P("node", None, "shard"), P("node", "shard", None)),
        check_vma=False,
    )
```

profile of v0, /device:TPU:1, one launch (start us, length us, event | category | flops | bytes accessed | tf_op | source)
XLA Modules:
  0.0 297.2 jit_solution(14384840601701058965)
XLA Ops:
  7.2 0.0 copy-start.3
  7.2 0.0 all-gather.2.cloned.1.call-start
  7.2 2.5 pad_maximum_fusion
  9.7 0.0 all-gather.2.cloned.1.call-update
  11.8 52.9 %all-gather.2.cloned.1.call-done = bf16[2,1024,1152]{2,1,0:T(8,128)(2,1)} async-done(((bf16[2,256,1152]{2,1,0:T(8,128)(2,1)}), bf16[2,1024,1152]{2,1,0:T(8,128)(2,1)}) %all-gather.2.cloned.1.call-update) | async-done | bytes 4718608 | tf_op jit(solution)/shard_map/all_gather | solution.py:23
  64.7 0.0 slice-start
  64.7 2.3 fusion.14
  67.1 0.0 copy-done.3
  67.1 0.0 slice-start.1
  67.1 0.0 copy-start.5
  67.1 5.4 %fusion.32 = f32[1024,1152]{1,0:T(8,128)S(1)} fusion(bf16[1,1152,1152]{2,1,0:T(8,128)(2,1)S(1)} %copy-done.3, f32[1024]{0:T(1024)S(1)} %add_rsqrt_fusion, bf16[2,1024,1152]{2,1,0:T(8,128)(2,1)} %all-gather.2.cloned.1.call-done), kind=kOutput, calls=%fused_computation.45 | convolution fusion | flops 2721447936 | bytes 9736192 | tf_op jit(solution)/shard_map/dot_general | solution.py:39
  72.5 0.0 slice-done
  72.5 0.0 slice-done.1
  72.5 0.0 copy-done.5
  72.5 0.0 copy-start.2
  72.5 3.6 %fusion.28 = f32[1024,1152]{1,0:T(8,128)S(1)} fusion(bf16[1,1152,1152]{2,1,0:T(8,128)(2,1)S(1)} %copy-done.5, f32[1024]{0:T(1024)S(1)} %add_rsqrt_fusion, bf16[2,1024,1152]{2,1,0:T(8,128)(2,1)S(1)} %bitcast.45), kind=kOutput, calls=%fused_computation.41 | convolution fusion | flops 2721447936 | bytes 9736192 | tf_op jit(solution)/shard_map/dot_general | solution.py:40
  76.1 0.0 copy-done.2
  76.1 0.0 copy-start.6
  76.1 5.5 %fusion.30 = f32[1024,1152]{1,0:T(8,128)} fusion(bf16[1,1152,1152]{2,1,0:T(8,128)(2,1)S(1)} %copy-done.2, pred[1024]{0:T(1024)(128)(4,1)S(1)} %fusion.48, bf16[2,1024,1152]{2,1,0:T(8,128)(2,1)S(1)} %bitcast.45), kind=kOutput, calls=%fused_computation.43 | convolution fusion | flops 2719088640 | bytes 9733120 | tf_op jit(solution)/shard_map/dot_general | solution.py:44
  81.6 0.0 copy-done.6
  81.6 0.0 copy-start.4
  81.6 4.4 %fusion.3 = bf16[1152,1152]{1,0:T(8,128)(2,1)S(1)} fusion(bf16[1,1152,1152]{2,1,0:T(8,128)(2,1)S(1)} %copy-done.2, f32[]{:T(128)} %bitcast.1, f32[1024,1152]{1,0:T(8,128)S(1)} %fusion.28, pred[1024]{0:T(1024)(128)(4,1)S(1)} %fusion.48, f32[1024,1152]{1,0:T(8,128)S(1)} %fusion.32, bf16[2,1024,1152]{2,1,0:T(8,128)(2,1)S(1)} %bitcast.45), kind=kOutput, calls=%fused_computation.6 | convolution fusion | flops 2736193536 | bytes 17105924 | tf_op jit(solution)/shard_map/dot_general | solution.py:52
  86.1 0.0 copy-done.4
  86.1 9.1 %fusion.5 = bf16[1152,1152]{1,0:T(8,128)(2,1)S(1)} fusion(bf16[1,1152,1152]{2,1,0:T(8,128)(2,1)S(1)} %copy-done.4, f32[]{:T(128)} %bitcast.1, f32[1024,1152]{1,0:T(8,128)S(1)} %fusion.32, f32[1024,1152]{1,0:T(8,128)} %fusion.30, f32[1024,1152]{1,0:T(8,128)} %copy-done.6, f32[1024]{0:T(1024)S(1)} %add_rsqrt_fusion, bf16[2,1024,1152]{2,1,0:T(8,128)(2,1)S(1)} %bitcast.45), kind=kOutput, calls=%fused_computation.8 | convolution fusion | flops 2750349312 | bytes 21827588 | tf_op jit(solution)/shard_map/dot_general | solution.py:50
  95.1 0.0 copy-start
  95.2 8.8 %fusion.4 = bf16[1152,1152]{1,0:T(8,128)(2,1)} fusion(bf16[1,1152,1152]{2,1,0:T(8,128)(2,1)S(1)} %copy-done.5, f32[]{:T(128)} %bitcast.1, f32[1024,1152]{1,0:T(8,128)} %fusion.30, f32[1024,1152]{1,0:T(8,128)S(1)} %fusion.32, f32[1024]{0:T(1024)S(1)} %add_rsqrt_fusion, bf16[2,1024,1152]{2,1,0:T(8,128)(2,1)S(1)} %bitcast.45), kind=kOutput, calls=%fused_computation.7 | convolution fusion | flops 2738552832 | bytes 17108996 | tf_op jit(solution)/shard_map/dot_general | solution.py:51
  104.0 0.0 copy-done
  104.0 174.8 %conditional.4 = (bf16[1152,1152]{1,0:T(8,128)(2,1)}, bf16[1152,1152]{1,0:T(8,128)(2,1)}, bf16[1152,1152]{1,0:T(8,128)(2,1)}) conditional(s32[]{:T(128)} %clamp.3, (bf16[1152,1152]{1,0:T(8,128)(2,1)S(1)}, bf16[1152,1152]{1,0:T(8,128)(2,1)}, bf16[1152,1152]{1,0:T(8,128)(2,1)S(1)}) %tuple.70, ...), branch_computations={%region_1.2_spmd, %region_2.3_spmd, %region_3.4_spmd, %region_4.5_... | conditional | bytes 31850640
  104.0 2.9 collective-permute-start.9
  106.8 0.1 collective-permute-start.10
  106.9 2.9 collective-permute-start.11
  109.8 55.3 %collective-permute-done.9 = bf16[1152,1152]{1,0:T(8,128)(2,1)} collective-permute-done((bf16[1152,1152]{1,0:T(8,128)(2,1)S(1)}, bf16[1152,1152]{1,0:T(8,128)(2,1)}, u32[]{:S(2)}, u32[]{:S(2)}) %collective-permute-start.9) | collective-permute-done | bytes 2654240 | tf_op jit(solution)/shard_map/cond/branch_3_fun/ppermute | solution.py:18
  165.1 56.9 %collective-permute-done.10 = bf16[1152,1152]{1,0:T(8,128)(2,1)} collective-permute-done((bf16[1152,1152]{1,0:T(8,128)(2,1)}, bf16[1152,1152]{1,0:T(8,128)(2,1)}, u32[]{:S(2)}, u32[]{:S(2)}) %collective-permute-start.10) | collective-permute-done | bytes 2654240 | tf_op jit(solution)/shard_map/cond/branch_3_fun/ppermute | solution.py:18
  222.0 56.7 %collective-permute-done.11 = bf16[1152,1152]{1,0:T(8,128)(2,1)} collective-permute-done((bf16[1152,1152]{1,0:T(8,128)(2,1)S(1)}, bf16[1152,1152]{1,0:T(8,128)(2,1)}, u32[]{:S(2)}, u32[]{:S(2)}) %collective-permute-start.11) | collective-permute-done | bytes 2654240 | tf_op jit(solution)/shard_map/cond/branch_3_fun/ppermute | solution.py:18
  278.8 0.0 copy-start.1
  278.8 4.2 %fusion.27 = bf16[1,1152,1152]{2,1,0:T(8,128)(2,1)} fusion(bf16[1152,1152]{1,0:T(8,128)(2,1)} %get-tuple-element.80, bf16[1152,1152]{1,0:T(8,128)(2,1)S(1)} %fusion.3), kind=kLoop, calls=%fused_computation.40 | loop fusion | flops 6635520 | bytes 7962624 | tf_op jit(solution)/shard_map/broadcast_in_dim | solution.py:94
  283.0 0.0 copy-done.1
  283.0 7.4 %fusion.25 = (bf16[1,1152,1152]{2,1,0:T(8,128)(2,1)}, bf16[1,1152,1152]{2,1,0:T(8,128)(2,1)}) fusion(bf16[1152,1152]{1,0:T(8,128)(2,1)} %get-tuple-element.78, bf16[1152,1152]{1,0:T(8,128)(2,1)S(1)} %copy-done.1, bf16[1152,1152]{1,0:T(8,128)(2,1)} %get-tuple-element.79, bf16[1152,1152]{1,0:T(8,128)(2,1)} %fusion.4), kind=kLoop, calls=%fused_computation.38 | loop fusion | flops 13271040 | bytes 15925248 | tf_op jit(solution)/shard_map/broadcast_in_dim | solution.py:94
  (3 shorter events, 0.0 us)
Async XLA Ops:
  7.2 59.9 %copy-start.3 = (bf16[1,1152,1152]{2,1,0:T(8,128)(2,1)S(1)}, bf16[1,1152,1152]{2,1,0:T(8,128)(2,1)}, u32[]{:S(2)}) copy-start(bf16[1,1152,1152]{2,1,0:T(8,128)(2,1)} %param.18) | copy-start | bytes 7962628
  7.2 57.5 %all-gather.2.cloned.1.call-start = ((), (), s32[]{:S(2)}) async-start(), calls=%async_computation | async-start | bytes 5898240 | tf_op jit(solution)/shard_map/all_gather | solution.py:23
  64.7 7.8 %slice-start = ((s8[4718592]{0:T(1024)(128)(4,1)}), s8[4194304]{0:T(1024)(128)(4,1)S(1)}, s32[]{:S(2)}) async-start(s8[4718592]{0:T(1024)(128)(4,1)} %bitcast.44), calls=%async_computation.1 | async-start | bytes 8388608
  67.1 5.4 %slice-start.1 = ((s8[4718592]{0:T(1024)(128)(4,1)}), s8[524288]{0:T(1024)(128)(4,1)S(1)}, s32[]{:S(2)}) async-start(s8[4718592]{0:T(1024)(128)(4,1)} %bitcast.44), calls=%async_computation.2 | async-start | bytes 1048576
  67.1 5.4 %copy-start.5 = (bf16[1,1152,1152]{2,1,0:T(8,128)(2,1)S(1)}, bf16[1,1152,1152]{2,1,0:T(8,128)(2,1)}, u32[]{:S(2)}) copy-start(bf16[1,1152,1152]{2,1,0:T(8,128)(2,1)} %param.19) | copy-start | bytes 7962628
  72.5 3.6 %copy-start.2 = (bf16[1,1152,1152]{2,1,0:T(8,128)(2,1)S(1)}, bf16[1,1152,1152]{2,1,0:T(8,128)(2,1)}, u32[]{:S(2)}) copy-start(bf16[1,1152,1152]{2,1,0:T(8,128)(2,1)} %param.20) | copy-start | bytes 7962628
  76.1 5.5 %copy-start.6 = (f32[1024,1152]{1,0:T(8,128)}, f32[1024,1152]{1,0:T(8,128)S(1)}, u32[]{:S(2)}) copy-start(f32[1024,1152]{1,0:T(8,128)S(1)} %fusion.28) | copy-start | bytes 14155780
  81.6 4.4 %copy-start.4 = (bf16[1,1152,1152]{2,1,0:T(8,128)(2,1)S(1)}, bf16[1,1152,1152]{2,1,0:T(8,128)(2,1)}, u32[]{:S(2)}) copy-start(bf16[1,1152,1152]{2,1,0:T(8,128)(2,1)} %param.18) | copy-start | bytes 7962628
  95.1 8.8 %copy-start = (bf16[1152,1152]{1,0:T(8,128)(2,1)}, bf16[1152,1152]{1,0:T(8,128)(2,1)S(1)}, u32[]{:S(2)}) copy-start(bf16[1152,1152]{1,0:T(8,128)(2,1)S(1)} %fusion.5) | copy-start | bytes 7962628
  104.0 61.2 %collective-permute-start.9 = (bf16[1152,1152]{1,0:T(8,128)(2,1)S(1)}, bf16[1152,1152]{1,0:T(8,128)(2,1)}, u32[]{:S(2)}, u32[]{:S(2)}) collective-permute-start(bf16[1152,1152]{1,0:T(8,128)(2,1)S(1)} %get-tuple-element.57), channel_id=1, source_target_pairs={{0,32},{4,36},{8,40},{12,44},{16,48},{20,52},{24,56},{28,60},{32,0... | collective-permute-start | bytes 7962632 | tf_op jit(solution)/shard_map/cond/branch_3_fun/ppermute | solution.py:18
  106.8 115.2 %collective-permute-start.10 = (bf16[1152,1152]{1,0:T(8,128)(2,1)}, bf16[1152,1152]{1,0:T(8,128)(2,1)}, u32[]{:S(2)}, u32[]{:S(2)}) collective-permute-start(bf16[1152,1152]{1,0:T(8,128)(2,1)} %get-tuple-element.58), channel_id=1, source_target_pairs={{0,32},{4,36},{8,40},{12,44},{16,48},{20,52},{24,56},{28,60},{32,0... | collective-permute-start | bytes 7962632 | tf_op jit(solution)/shard_map/cond/branch_3_fun/ppermute | solution.py:18
  106.9 171.8 %collective-permute-start.11 = (bf16[1152,1152]{1,0:T(8,128)(2,1)S(1)}, bf16[1152,1152]{1,0:T(8,128)(2,1)}, u32[]{:S(2)}, u32[]{:S(2)}) collective-permute-start(bf16[1152,1152]{1,0:T(8,128)(2,1)S(1)} %get-tuple-element.59), channel_id=1, source_target_pairs={{0,32},{4,36},{8,40},{12,44},{16,48},{20,52},{24,56},{28,60},{32,0... | collective-permute-start | bytes 7962632 | tf_op jit(solution)/shard_map/cond/branch_3_fun/ppermute | solution.py:18
  278.8 4.2 %copy-start.1 = (bf16[1152,1152]{1,0:T(8,128)(2,1)S(1)}, bf16[1152,1152]{1,0:T(8,128)(2,1)}, u32[]{:S(2)}) copy-start(bf16[1152,1152]{1,0:T(8,128)(2,1)} %copy-done) | copy-start | bytes 7962628
Sparse Core Ops, SparseCore 0:
  10.2 54.4 all-gather.1
where the time goes:
time: 297 us
  waiting for transfers between devices  222 us (75%)
  matrix products  36.7 us (12%)
  other arithmetic  16.5 us (6%)
  between operations  16.2 us (5%)
  starting transfers between devices  5.88 us (2%)
    ppermute x3, waiting for transfers between devices, partner(): lax.ppermute(array, axis, [(i, i ^ 1 << distance) for i in range(lax.axis...  169 us
    all_gather x1, waiting for transfers between devices, sent_together(): lax.all_gather(both, axis, axis=dim, tiled=True)  52.9 us
    broadcast_in_dim x2, other arithmetic, per_device(): return (mixed[0][None], mixed[1][None], mixed[2][None])  11.6 us
    dot_general x1, matrix products, slot_grads(): lax.dot_general(normed, d_gate, inner, preferred_element_type=jnp.float32)  9.06 us
    dot_general x1, matrix products, slot_grads(): lax.dot_general(normed, d_up, inner, preferred_element_type=jnp.float32)  8.79 us
  transfers between devices with their start and end apart: 4, of which 4 were waited for; matrix products, arithmetic and copies ran while one was open for 0% of the time, Pallas kernels for 0%

commit v1 on v0

v1 whole, which is shorter than its diff:
```python
import functools

import jax
import jax.numpy as jnp
from jax import lax
from jax.experimental import pallas as pl
from jax.experimental.pallas import tpu as pltpu
from jax.sharding import PartitionSpec as P

MESH = pl.DeviceIdType.MESH
CHUNK = 128
PIECES = 4
BLOCK = 128


def remote(src, dst, send_sem, recv_sem, device):
    return pltpu.make_async_remote_copy(
        src_ref=src,
        dst_ref=dst,
        send_sem=send_sem,
        recv_sem=recv_sem,
        device_id=device,
        device_id_type=MESH,
    )


def round_kernel(
    level,
    count_ref,
    step_ref,
    x_hbm,
    g_hbm,
    wg_hbm,
    wu_hbm,
    wd_hbm,
    mixed_gate,
    mixed_up,
    mixed_down,
    raw,
    normed,
    normed_t,
    grad_out,
    w_gate,
    w_up,
    w_down,
    d_both,
    hidden,
    own_gate,
    own_up,
    own_down,
    got_gate,
    got_up,
    got_down,
    local_sem,
    near_send,
    near_recv,
    far_send,
    far_recv,
    relay_send,
    relay_recv,
    chunk_send,
    chunk_recv,
    out_sem,
):
    node, shard = lax.axis_index("node"), lax.axis_index("shard")
    core, chip = lax.rem(shard, 2), shard // 2
    near = (node, chip * 2 + 1 - core)
    far = (node, (1 - chip) * 2 + core)
    stride = 1 << level
    peer = (node + (1 - 2 * lax.rem(node // stride, 2)) * stride, shard)
    seq = raw.shape[2]
    rows, width = normed.shape
    piece = seq // PIECES
    n_chunks = own_gate.shape[0]

    def load(i, src, dst):
        return pltpu.make_async_copy(src, dst, local_sem.at[i])

    loads = [
        load(0, x_hbm, raw.at[0, 0]),
        load(1, g_hbm, raw.at[1, 0]),
        load(2, wg_hbm, w_gate),
        load(3, wu_hbm, w_up),
        load(4, wd_hbm, w_down),
    ]
    for copy in loads:
        copy.start()

    barrier = pltpu.get_barrier_semaphore()
    for device in (near, far, peer):
        pl.semaphore_signal(barrier, inc=1, device_id=device, device_id_type=MESH)
    pl.semaphore_wait(barrier, 3)

    def to_far(kind, i):
        at = pl.ds(i * piece, piece)
        return remote(
            raw.at[kind, 0, at], raw.at[kind, 2, at], far_send.at[kind, i], far_recv.at[kind, i], far
        )

    def to_near(kind, i):
        at = pl.ds(i * piece, piece)
        return remote(
            raw.at[kind, 0, at], raw.at[kind, 1, at], near_send.at[kind, i], near_recv.at[kind, i], near
        )

    def relay(kind, i):
        at = pl.ds(i * piece, piece)
        return remote(
            raw.at[kind, 2, at], raw.at[kind, 3, at], relay_send.at[kind, i], relay_recv.at[kind, i], near
        )

    both = [(kind, i) for i in range(PIECES) for kind in range(2)]
    loads[0].wait()
    loads[1].wait()
    for kind, i in both:
        to_far(kind, i).start()
    for kind, i in both:
        to_near(kind, i).start()

    def prepare(slot, start):
        at = pl.ds(start, BLOCK)
        to = pl.ds(pl.multiple_of(slot * seq + start, BLOCK), BLOCK)
        floats = raw[0, slot, at].astype(jnp.float32)
        scale = lax.rsqrt(jnp.mean(floats * floats, -1, keepdims=True) + 1e-06)
        value = (floats * scale).astype(jnp.bfloat16)
        normed[to] = value
        normed_t[:, to] = value.T
        live = jnp.where(lax.bitwise_xor(shard, slot) < count_ref[0], 1.0, 0.0)
        grad_out[to] = (raw[1, slot, at].astype(jnp.float32) * live).astype(jnp.bfloat16)

    def prepare_slot(slot):
        @pl.loop(0, seq // BLOCK)
        def _(i):
            prepare(slot, pl.multiple_of(i * BLOCK, BLOCK))

    prepare_slot(0)
    for kind, i in both:
        to_near(kind, i).wait_recv()
    prepare_slot(1)
    for kind, i in both:
        to_far(kind, i).wait_recv()
        relay(kind, i).start()
    prepare_slot(2)
    for kind, i in both:
        relay(kind, i).wait_recv()
    prepare_slot(3)
    for copy in loads[2:]:
        copy.wait()

    step = step_ref[0]
    third = width // 3

    def sends(c):
        return [
            remote(mine.at[c], theirs.at[c], chunk_send.at[k, c], chunk_recv.at[k, c], peer)
            for k, (mine, theirs) in enumerate(
                ((own_gate, got_gate), (own_up, got_up), (own_down, got_down))
            )
        ]

    @pl.loop(0, n_chunks)
    def _(c):
        units = pl.ds(pl.multiple_of(c * CHUNK, CHUNK), CHUNK)

        @pl.loop(0, rows // seq)
        def _(r):
            at = pl.ds(pl.multiple_of(r * seq, seq), seq)
            n = normed[at]
            gate = jnp.dot(n, w_gate[:, units], preferred_element_type=jnp.float32)
            up = jnp.dot(n, w_up[:, units], preferred_element_type=jnp.float32)
            back = lax.dot_general(
                grad_out[at],
                w_down[units],
                (((1,), (1,)), ((), ())),
                preferred_element_type=jnp.float32,
            )
            k = 0.7978845608028654
            square = gate * gate
            t = jnp.tanh(gate * (k + (k * 0.044715) * square))
            half = 0.5 + 0.5 * t
            act = gate * half
            slope = half + (0.5 * gate) * (1.0 - t * t) * (k + (3.0 * k * 0.044715) * square)
            hidden[at] = (act * up).astype(jnp.bfloat16)
            d_both[at, :CHUNK] = (back * up * slope).astype(jnp.bfloat16)
            d_both[at, CHUNK:] = (back * act).astype(jnp.bfloat16)

        @pl.loop(0, 3)
        def _(b):
            at = pl.ds(pl.multiple_of(b * third, third), third)
            grad = jnp.dot(normed_t[at], d_both[...], preferred_element_type=jnp.float32)
            own_gate[c, at] = (
                w_gate[at, units].astype(jnp.float32) - step * grad[:, :CHUNK]
            ).astype(jnp.bfloat16)
            own_up[c, at] = (
                w_up[at, units].astype(jnp.float32) - step * grad[:, CHUNK:]
            ).astype(jnp.bfloat16)

        hidden_t = hidden[...].T

        @pl.loop(0, 3)
        def _(b):
            at = pl.ds(pl.multiple_of(b * third, third), third)
            grad = jnp.dot(hidden_t, grad_out[:, at], preferred_element_type=jnp.float32)
            own_down[c, :, at] = (
                w_down[units, at].astype(jnp.float32) - step * grad
            ).astype(jnp.bfloat16)

        for copy in sends(c):
            copy.start()

    def writes(c):
        units = pl.ds(pl.multiple_of(c * CHUNK, CHUNK), CHUNK)
        return [
            pltpu.make_async_copy(got_gate.at[c], mixed_gate.at[:, units], out_sem.at[0, c]),
            pltpu.make_async_copy(got_up.at[c], mixed_up.at[:, units], out_sem.at[1, c]),
            pltpu.make_async_copy(got_down.at[c], mixed_down.at[units], out_sem.at[2, c]),
        ]

    def average(mine, theirs):
        theirs[...] = (
            0.5 * (mine[...].astype(jnp.float32) + theirs[...].astype(jnp.float32))
        ).astype(jnp.bfloat16)

    @pl.loop(0, n_chunks)
    def _(c):
        for copy, write, mine, theirs in zip(
            sends(c),
            writes(c),
            (own_gate, own_up, own_down),
            (got_gate, got_up, got_down),
        ):
            copy.wait_recv()
            average(mine.at[c], theirs.at[c])
            write.start()

    @pl.loop(0, n_chunks)
    def _(c):
        for copy, write in zip(sends(c), writes(c)):
            copy.wait_send()
            write.wait()

    for kind, i in both:
        to_far(kind, i).wait_send()
        to_near(kind, i).wait_send()
        relay(kind, i).wait_send()


def one_level(level, count, step, x, g, w_gate, w_up, w_down):
    seq, width = x.shape
    units = w_gate.shape[1]
    n_chunks, rows = units // CHUNK, 4 * seq
    bf16 = jnp.bfloat16
    hbm = pl.BlockSpec(memory_space=pltpu.HBM)
    smem = pl.BlockSpec(memory_space=pltpu.SMEM)
    dma = pltpu.SemaphoreType.DMA
    across = pltpu.VMEM((n_chunks, width, CHUNK), bf16)
    along = pltpu.VMEM((n_chunks, CHUNK, width), bf16)
    return pl.pallas_call(
        functools.partial(round_kernel, level),
        out_shape=[jax.ShapeDtypeStruct(w.shape, bf16) for w in (w_gate, w_up, w_down)],
        in_specs=[smem, smem] + [hbm] * 5,
        out_specs=[hbm] * 3,
        scratch_shapes=[
            pltpu.VMEM((2, 4, seq, width), bf16),
            pltpu.VMEM((rows, width), bf16),
            pltpu.VMEM((width, rows), bf16),
            pltpu.VMEM((rows, width), bf16),
            pltpu.VMEM(w_gate.shape, bf16),
            pltpu.VMEM(w_up.shape, bf16),
            pltpu.VMEM(w_down.shape, bf16),
            pltpu.VMEM((rows, 2 * CHUNK), bf16),
            pltpu.VMEM((rows, CHUNK), bf16),
            across,
            across,
            along,
            across,
            across,
            along,
            dma((5,)),
            dma((2, PIECES)),
            dma((2, PIECES)),
            dma((2, PIECES)),
            dma((2, PIECES)),
            dma((2, PIECES)),
            dma((2, PIECES)),
            dma((3, n_chunks)),
            dma((3, n_chunks)),
            dma((3, n_chunks)),
        ],
        compiler_params=pltpu.CompilerParams(
            collective_id=level, has_side_effects=True, vmem_limit_bytes=56 << 20
        ),
        cost_estimate=pl.CostEstimate(
            flops=12 * rows * width * units,
            bytes_accessed=2 * (6 * width * units + 2 * seq * width),
            transcendentals=rows * units,
        ),
        name=f"round_level_{level}",
    )(count, step, x, g, w_gate, w_up, w_down)


def per_device(inputs, upstream, counts, round_index, rates, gate_weight, up_weight, down_weight):
    step = rates * (250.0 / (250.0 + round_index.astype(jnp.float32)))
    levels = lax.axis_size("node").bit_length() - 1
    mixed = lax.switch(
        round_index[0] % levels,
        [functools.partial(one_level, level) for level in range(levels)],
        counts,
        step,
        inputs[0],
        upstream[0],
        gate_weight[0],
        up_weight[0],
        down_weight[0],
    )
    return tuple(m[None] for m in mixed)


def solution(mesh):
    return jax.shard_map(
        per_device,
        mesh=mesh,
        in_specs=(
            P("node", "shard", None),
            P("node", "shard", None),
            P("node"),
            P(),
            P("node"),
            P("node", None, "shard"),
            P("node", None, "shard"),
            P("node", "shard", None),
        ),
        out_specs=(P("node", None, "shard"), P("node", None, "shard"), P("node", "shard", None)),
        check_vma=False,
    )
```

time: 297 us -> 223 us (0.75)
  waiting for transfers between devices: 222 us -> 0 us
  Pallas kernels: 0 us -> 214 us
  matrix products: 36.7 us -> 0 us
  other arithmetic: 16.5 us -> 0 us
  between operations: 16.2 us -> 1.99 us
  starting transfers between devices: 5.88 us -> 0 us
  local copies, waits for them, and re-layouts: 0.05 us -> 5.71 us
    pallas_call x0 -> x1, Pallas kernels: none -> 214 us  [one_level(): pl.pallas_call(functools.partial(round_kernel, level), out_shape=[jax.Sha...]
    ppermute x3 -> x0, waiting for transfers between devices: 169 us -> none  [partner(): lax.ppermute(array, axis, [(i, i ^ 1 << distance) for i in range(lax.axis...]
    all_gather x1 -> x0, waiting for transfers between devices: 52.9 us -> none  [sent_together(): lax.all_gather(both, axis, axis=dim, tiled=True)]
    dot_general x6 -> x0, matrix products: 36.7 us -> none  [the longest x1 9.06 us: slot_grads(): lax.dot_general(normed, d_gate, inner, preferred_element_type=jnp.float32)]
    broadcast_in_dim x2 -> x0, other arithmetic: 11.6 us -> none  [per_device(): return (mixed[0][None], mixed[1][None], mixed[2][None])]
    ppermute x3 -> x0, starting transfers between devices: 5.84 us -> none  [partner(): lax.ppermute(array, axis, [(i, i ^ 1 << distance) for i in range(lax.axis...]
    unnamed x18 -> x5, local copies, waits for them, and re-layouts: 0.05 us -> 5.71 us
  transfers between devices with their start and end apart: 4 -> 0, of which waited for: 4 -> 0; matrix products, arithmetic and copies ran while one was open for 0% -> 0% of each run, Pallas kernels for 0% -> 0%
where the time goes in v1:
time: 223 us
  Pallas kernels  214 us (96%)
  local copies, waits for them, and re-layouts  5.71 us (3%)
    pallas_call x1, Pallas kernels, one_level(): pl.pallas_call(functools.partial(round_kernel, level), out_shape=[jax.Sha...  214 us
    unnamed x5, local copies, waits for them, and re-layouts  5.71 us

profile of v1, /device:TPU:1, one launch (start us, length us, event | category | flops | bytes accessed | tf_op | source)
XLA Modules:
  0.0 222.6 jit_solution(9760433614638468189)
XLA Ops:
  2.0 214.9 %conditional.1 = ((bf16[1152,1152]{1,0:T(8,128)(2,1)S(1)}, bf16[1152,1152]{1,0:T(8,128)(2,1)S(1)}, bf16[1152,1152]{1,0:T(8,128)(2,1)})) conditional(s32[]{:T(128)} %clamp.3, (s32[1]{0:T(128)}, f32[1]{0:T(128)}, bf16[256,1152]{1,0:T(8,128)(2,1)}, bf16[256,1152]{1,0:T(8,128)(2,1)}, bf16[1152,1152]{1,0:T(8,128)(2,1)}, ...), branch_computations={%region_0.1_spmd, %region_1.2_spmd, %region_2.3_spmd, %region_3.4_... | conditional | flops 16307453952 | bytes 17104904 | solution.py:305
  2.2 214.4 %round_level_3.1 = (bf16[1152,1152]{1,0:T(8,128)(2,1)S(1)}, bf16[1152,1152]{1,0:T(8,128)(2,1)S(1)}, bf16[1152,1152]{1,0:T(8,128)(2,1)}) custom-call(s32[1]{0:T(128)} %get-tuple-element.118.count_ref, f32[1]{0:T(128)} %get-tuple-element.119.step_ref, bf16[256,1152]{1,0:T(8,128)(2,1)} %get-tuple-element.120.x_hbm, bf16[256,1152]{1,0:T(8,128)(2,1)} %get-tuple-element.121.g_hbm, ...), custom_call_target="tpu_custom_call" | custom-call | flops 16307453952 | bytes 17104896 | tf_op jit(solution)/shard_map/cond/branch_3_fun/round_level_3/pallas_call | solution.py:258
  216.9 1.5 copy.31
  218.4 0.0 copy-start
  218.4 1.5 copy.32
  219.9 1.2 copy-done
  221.1 1.5 copy.33
Async XLA Ops:
  218.4 2.7 %copy-start = (bf16[1152,1152]{1,0:T(8,128)(2,1)S(1)}, bf16[1152,1152]{1,0:T(8,128)(2,1)}, u32[]{:S(2)}) copy-start(bf16[1152,1152]{1,0:T(8,128)(2,1)} %get-tuple-element.142) | copy-start | bytes 7962628

commit v2 on v1

v2 whole, which is shorter than its diff:
```python
import functools

import jax
import jax.numpy as jnp
from jax import lax
from jax.experimental import pallas as pl
from jax.experimental.pallas import tpu as pltpu
from jax.sharding import PartitionSpec as P

MESH = pl.DeviceIdType.MESH
CHUNK = 128
BLOCK = 128
PARTS = 3


def remote(src, dst, send_sem, recv_sem, device):
    return pltpu.make_async_remote_copy(
        src_ref=src,
        dst_ref=dst,
        send_sem=send_sem,
        recv_sem=recv_sem,
        device_id=device,
        device_id_type=MESH,
    )


def round_kernel(
    level,
    count_hbm,
    round_hbm,
    rate_hbm,
    x_hbm,
    g_hbm,
    wg_hbm,
    wu_hbm,
    wd_hbm,
    mixed_gate,
    mixed_up,
    mixed_down,
    raw,
    normed,
    normed_t,
    grad_out,
    w_gate,
    w_up,
    w_down,
    d_both,
    hidden,
    own_gate,
    own_up,
    own_down,
    got_gate,
    got_up,
    got_down,
    count_ref,
    round_ref,
    rate_ref,
    local_sem,
    near_send,
    near_recv,
    far_send,
    far_recv,
    relay_send,
    relay_recv,
    chunk_send,
    chunk_recv,
):
    node, shard = lax.axis_index("node"), lax.axis_index("shard")
    core, chip = lax.rem(shard, 2), shard // 2
    near = (node, chip * 2 + 1 - core)
    far = (node, (1 - chip) * 2 + core)
    stride = 1 << level
    peer = (node + (1 - 2 * lax.rem(node // stride, 2)) * stride, shard)
    n_blocks = raw.shape[1]
    width = normed.shape[1]
    n_chunks = own_gate.shape[0]

    def load(i, src, dst):
        return pltpu.make_async_copy(src, dst, local_sem.at[i])

    def rows_of(h):
        return pl.ds(h * BLOCK, BLOCK)

    slot_loads = [
        load(kind * 2 + h, src.at[rows_of(h)], raw.at[kind, h])
        for h in range(2)
        for kind, src in enumerate((x_hbm, g_hbm))
    ]
    other_loads = [
        load(4, wg_hbm, w_gate),
        load(5, wu_hbm, w_up),
        load(6, wd_hbm, w_down),
        load(7, count_hbm, count_ref),
        load(8, round_hbm, round_ref),
        load(9, rate_hbm, rate_ref),
    ]
    for copy in slot_loads + other_loads:
        copy.start()

    barrier = pltpu.get_barrier_semaphore()
    for device in (near, far, peer):
        pl.semaphore_signal(barrier, inc=1, device_id=device, device_id_type=MESH)
    pl.semaphore_wait(barrier, 3)

    def to_near(kind, h):
        return remote(
            raw.at[kind, h], raw.at[kind, 2 + h], near_send.at[kind, h], near_recv.at[kind, h], near
        )

    def to_far(kind, h):
        return remote(
            raw.at[kind, h], raw.at[kind, 4 + 2 * h], far_send.at[kind, h], far_recv.at[kind, h], far
        )

    def relay(kind, h):
        return remote(
            raw.at[kind, 4 + 2 * h],
            raw.at[kind, 5 + 2 * h],
            relay_send.at[kind, h],
            relay_recv.at[kind, h],
            near,
        )

    both = [(kind, h) for h in range(2) for kind in range(2)]
    for copy, (kind, h) in zip(slot_loads, both):
        copy.wait()
        to_far(kind, h).start()
    for kind, h in both:
        to_near(kind, h).start()
    for copy in other_loads:
        copy.wait()

    decay = 250.0 / (250.0 + jnp.full((8, 128), round_ref[0], jnp.int32).astype(jnp.float32))
    step = jnp.max(rate_ref[0] * decay)

    def prepare(block):
        to = pl.ds(pl.multiple_of(block * BLOCK, BLOCK), BLOCK)
        floats = raw[0, block].astype(jnp.float32)
        scale = lax.rsqrt(jnp.mean(floats * floats, -1, keepdims=True) + 1e-06)
        value = (floats * scale).astype(jnp.bfloat16)
        normed[to] = value
        normed_t[:, to] = value.T
        slot = lax.bitwise_xor(shard, jnp.where(block < 4, block // 2, 2 + lax.rem(block, 2)))
        live = jnp.where(slot < count_ref[0], 1.0, 0.0)
        grad_out[to] = (raw[1, block].astype(jnp.float32) * live).astype(jnp.bfloat16)

    def units_of(c):
        return pl.ds(pl.multiple_of(c * CHUNK, CHUNK), CHUNK)

    def forward(c, block):
        units = units_of(c)
        at = pl.ds(pl.multiple_of(block * BLOCK, BLOCK), BLOCK)
        n = normed[at]
        gate = jnp.dot(n, w_gate[:, units], preferred_element_type=jnp.float32)
        up = jnp.dot(n, w_up[:, units], preferred_element_type=jnp.float32)
        back = lax.dot_general(
            grad_out[at],
            w_down[units],
            (((1,), (1,)), ((), ())),
            preferred_element_type=jnp.float32,
        )
        k = 0.7978845608028654
        square = gate * gate
        t = jnp.tanh(gate * (k + (k * 0.044715) * square))
        half = 0.5 + 0.5 * t
        act = gate * half
        slope = half + (0.5 * gate) * (1.0 - t * t) * (k + (3.0 * k * 0.044715) * square)
        hidden[at] = (act * up).astype(jnp.bfloat16)
        d_both[at, :CHUNK] = (back * up * slope).astype(jnp.bfloat16)
        d_both[at, CHUNK:] = (back * act).astype(jnp.bfloat16)

    @pl.loop(0, n_blocks)
    def _(block):
        @pl.when(block == 2)
        def _():
            for kind, h in both:
                to_near(kind, h).wait_recv()

        @pl.when((block >= 4) & (lax.rem(block, 2) == 0))
        def _():
            h = block // 2 - 2
            for kind in range(2):
                to_far(kind, h).wait_recv()
                relay(kind, h).start()

        @pl.when((block >= 4) & (lax.rem(block, 2) == 1))
        def _():
            h = block // 2 - 2
            for kind in range(2):
                relay(kind, h).wait_recv()

        prepare(block)
        forward(0, block)

    part = width // PARTS
    pairs = ((own_gate, got_gate), (own_up, got_up), (own_down, got_down))

    def sent(k, c, at=None):
        mine, theirs = (ref.at[c] if at is None else ref.at[c, at] for ref in pairs[k])
        return remote(mine, theirs, chunk_send.at[k, c], chunk_recv.at[k, c], peer)

    @pl.loop(0, n_chunks)
    def _(c):
        units = units_of(c)

        @pl.loop(0, PARTS)
        def _(b):
            at = pl.ds(pl.multiple_of(b * part, part), part)
            grad = jnp.dot(normed_t[at], d_both[...], preferred_element_type=jnp.float32)
            own_gate[c, at] = (
                w_gate[at, units].astype(jnp.float32) - step * grad[:, :CHUNK]
            ).astype(jnp.bfloat16)
            own_up[c, at] = (
                w_up[at, units].astype(jnp.float32) - step * grad[:, CHUNK:]
            ).astype(jnp.bfloat16)
            sent(0, c, at).start()
            sent(1, c, at).start()

        hidden_t = hidden[...].T

        @pl.loop(0, PARTS)
        def _(b):
            at = pl.ds(pl.multiple_of(b * part, part), part)
            grad = jnp.dot(hidden_t, grad_out[:, at], preferred_element_type=jnp.float32)
            own_down[c, :, at] = (
                w_down[units, at].astype(jnp.float32) - step * grad
            ).astype(jnp.bfloat16)

        sent(2, c).start()

        @pl.when(c < n_chunks - 1)
        def _():
            @pl.loop(0, n_blocks)
            def _(block):
                forward(c + 1, block)

    def average(mine, theirs):
        return (0.5 * (mine.astype(jnp.float32) + theirs.astype(jnp.float32))).astype(jnp.bfloat16)

    @pl.loop(0, n_chunks)
    def _(c):
        units = units_of(c)
        sent(0, c).wait_recv()
        mixed_gate[:, units] = average(own_gate[c], got_gate[c])
        sent(1, c).wait_recv()
        mixed_up[:, units] = average(own_up[c], got_up[c])
        sent(2, c).wait_recv()
        mixed_down[units] = average(own_down[c], got_down[c])

    @pl.loop(0, n_chunks)
    def _(c):
        for k in range(3):
            sent(k, c).wait_send()

    for kind, h in both:
        to_far(kind, h).wait_send()
        to_near(kind, h).wait_send()
        relay(kind, h).wait_send()


def one_level(level, count, round_index, rate, x, g, w_gate, w_up, w_down):
    seq, width = x.shape
    units = w_gate.shape[1]
    n_chunks, rows = units // CHUNK, 4 * seq
    bf16 = jnp.bfloat16
    hbm = pl.BlockSpec(memory_space=pltpu.HBM)
    vmem = pl.BlockSpec(memory_space=pltpu.VMEM)
    dma = pltpu.SemaphoreType.DMA
    across = pltpu.VMEM((n_chunks, width, CHUNK), bf16)
    along = pltpu.VMEM((n_chunks, CHUNK, width), bf16)
    mixed = pl.pallas_call(
        functools.partial(round_kernel, level),
        out_shape=[pltpu.VMEM(w.shape, bf16) for w in (w_gate, w_up, w_down)],
        in_specs=[hbm] * 8,
        out_specs=[vmem] * 3,
        scratch_shapes=[
            pltpu.VMEM((2, rows // BLOCK, BLOCK, width), bf16),
            pltpu.VMEM((rows, width), bf16),
            pltpu.VMEM((width, rows), bf16),
            pltpu.VMEM((rows, width), bf16),
            pltpu.VMEM(w_gate.shape, bf16),
            pltpu.VMEM(w_up.shape, bf16),
            pltpu.VMEM(w_down.shape, bf16),
            pltpu.VMEM((rows, 2 * CHUNK), bf16),
            pltpu.VMEM((rows, CHUNK), bf16),
            across,
            across,
            along,
            across,
            across,
            along,
            pltpu.SMEM((1,), jnp.int32),
            pltpu.SMEM((1,), jnp.int32),
            pltpu.SMEM((1,), jnp.float32),
            dma((10,)),
            dma((2, 2)),
            dma((2, 2)),
            dma((2, 2)),
            dma((2, 2)),
            dma((2, 2)),
            dma((2, 2)),
            dma((3, n_chunks)),
            dma((3, n_chunks)),
        ],
        compiler_params=pltpu.CompilerParams(
            collective_id=level, has_side_effects=True, vmem_limit_bytes=44 << 20
        ),
        cost_estimate=pl.CostEstimate(
            flops=12 * rows * width * units,
            bytes_accessed=2 * (6 * width * units + 2 * seq * width),
            transcendentals=rows * units,
        ),
        name=f"round_level_{level}",
    )(count, round_index, rate, x, g, w_gate, w_up, w_down)
    return write_out(*mixed)


def write_kernel(gate, up, down, out_gate, out_up, out_down, sem):
    copies = [
        pltpu.make_async_copy(src, dst, sem.at[i])
        for i, (src, dst) in enumerate(((gate, out_gate), (up, out_up), (down, out_down)))
    ]
    for copy in copies:
        copy.start()
    for copy in copies:
        copy.wait()


def write_out(*arrays):
    return pl.pallas_call(
        write_kernel,
        out_shape=[jax.ShapeDtypeStruct(a.shape, a.dtype) for a in arrays],
        in_specs=[pl.BlockSpec(memory_space=pltpu.VMEM)] * 3,
        out_specs=[pl.BlockSpec(memory_space=pltpu.HBM)] * 3,
        scratch_shapes=[pltpu.SemaphoreType.DMA((3,))],
        compiler_params=pltpu.CompilerParams(vmem_limit_bytes=16 << 20),
        name="write_out",
    )(*arrays)


def per_device(inputs, upstream, counts, round_index, rates, gate_weight, up_weight, down_weight):
    levels = lax.axis_size("node").bit_length() - 1
    mixed = lax.switch(
        lax.rem(round_index[0], levels),
        [functools.partial(one_level, level) for level in range(levels)],
        counts,
        round_index,
        rates,
        inputs[0],
        upstream[0],
        gate_weight[0],
        up_weight[0],
        down_weight[0],
    )
    return tuple(m[None] for m in mixed)


def solution(mesh):
    return jax.shard_map(
        per_device,
        mesh=mesh,
        in_specs=(
            P("node", "shard", None),
            P("node", "shard", None),
            P("node"),
            P(),
            P("node"),
            P("node", None, "shard"),
            P("node", None, "shard"),
            P("node", "shard", None),
        ),
        out_specs=(P("node", None, "shard"), P("node", None, "shard"), P("node", "shard", None)),
        check_vma=False,
    )
```

time: 223 us -> 214 us (0.960)
  local copies, waits for them, and re-layouts: 5.71 us -> 0 us
    unnamed x5 -> x0, local copies, waits for them, and re-layouts: 5.71 us -> none
    pallas_call x1 -> x2, Pallas kernels: 214 us -> 213 us  [the longest x1 210 us: one_level(): pl.pallas_call(functools.partial(round_kernel, level), out_shape=[pltpu.V...]
where the time goes in v2:
time: 214 us
  Pallas kernels  213 us (100%)
    pallas_call x1, Pallas kernels, one_level(): pl.pallas_call(functools.partial(round_kernel, level), out_shape=[pltpu.V...  210 us

profile of v2, /device:TPU:1, one launch (start us, length us, event | category | flops | bytes accessed | tf_op | source)
XLA Modules:
  0.0 214.3 jit_solution(14015971261958192835)
XLA Ops:
  1.3 213.0 %conditional.1 = ((bf16[1152,1152]{1,0:T(8,128)(2,1)}, bf16[1152,1152]{1,0:T(8,128)(2,1)}, bf16[1152,1152]{1,0:T(8,128)(2,1)})) conditional(s32[]{:T(128)} %bitcast, (s32[1]{0:T(128)}, s32[1]{0:T(128)}, f32[1]{0:T(128)}, bf16[256,1152]{1,0:T(8,128)(2,1)}, bf16[256,1152]{1,0:T(8,128)(2,1)}, ...), branch_computations={%region_0.0_spmd.clone, %region_1.0_spmd.clone, %region_2.0_spmd.c... | conditional | flops 16307453952 | bytes 17104904 | solution.py:343
  1.3 209.7 %round_level_3.1 = (bf16[1152,1152]{1,0:T(8,128)(2,1)S(1)}, bf16[1152,1152]{1,0:T(8,128)(2,1)S(1)}, bf16[1152,1152]{1,0:T(8,128)(2,1)S(1)}) custom-call(s32[1]{0:T(128)} %get-tuple-element.212.count_hbm, s32[1]{0:T(128)} %get-tuple-element.213.round_hbm, f32[1]{0:T(128)} %get-tuple-element.214.rate_hbm, bf16[256,1152]{1,0:T(8,128)(2,1)} %get-tuple-element.215.x_hbm, ...), custom_call_target="tpu_custom_call" | custom-call | flops 16307453952 | bytes 17104896 | tf_op jit(solution)/shard_map/cond/branch_3_fun/round_level_3/pallas_call | solution.py:271
  211.0 3.3 %write_out.8 = (bf16[1152,1152]{1,0:T(8,128)(2,1)}, bf16[1152,1152]{1,0:T(8,128)(2,1)}, bf16[1152,1152]{1,0:T(8,128)(2,1)}) custom-call(bf16[1152,1152]{1,0:T(8,128)(2,1)S(1)} %get-tuple-element.220.gate, bf16[1152,1152]{1,0:T(8,128)(2,1)S(1)} %get-tuple-element.221.up, bf16[1152,1152]{1,0:T(8,128)(2,1)S(1)} %get-tuple-element.222.down), custom_call_target="tpu_custom_call" | custom-call | tf_op jit(solution)/shard_map/cond/branch_3_fun/write_out/pallas_call | solution.py:330

commit v3 on v2

--- a/solution.py
+++ b/solution.py
@@ -26,6 +26,7 @@
 
 def round_kernel(
     level,
+    early,
     count_hbm,
     round_hbm,
     rate_hbm,
@@ -64,6 +65,7 @@
     relay_recv,
     chunk_send,
     chunk_recv,
+    *partner,
 ):
     node, shard = lax.axis_index("node"), lax.axis_index("shard")
     core, chip = lax.rem(shard, 2), shard // 2
@@ -102,60 +104,102 @@
         pl.semaphore_signal(barrier, inc=1, device_id=device, device_id_type=MESH)
     pl.semaphore_wait(barrier, 3)
 
-    def to_near(kind, h):
-        return remote(
-            raw.at[kind, h], raw.at[kind, 2 + h], near_send.at[kind, h], near_recv.at[kind, h], near
-        )
-
-    def to_far(kind, h):
-        return remote(
-            raw.at[kind, h], raw.at[kind, 4 + 2 * h], far_send.at[kind, h], far_recv.at[kind, h], far
-        )
-
-    def relay(kind, h):
-        return remote(
-            raw.at[kind, 4 + 2 * h],
-            raw.at[kind, 5 + 2 * h],
-            relay_send.at[kind, h],
-            relay_recv.at[kind, h],
-            near,
+    def hop(sems, blocks, start, stop, device):
+        def copy(kind, h):
+            return remote(
+                blocks.at[kind, start(h)],
+                blocks.at[kind, stop(h)],
+                sems[0].at[kind, h],
+                sems[1].at[kind, h],
+                device,
+            )
+
+        return copy
+
+    def hops(near_sems, far_sems, relay_sems, blocks):
+        return (
+            hop(near_sems, blocks, lambda h: h, lambda h: 2 + h, near),
+            hop(far_sems, blocks, lambda h: h, lambda h: 4 + 2 * h, far),
+            hop(relay_sems, blocks, lambda h: 4 + 2 * h, lambda h: 5 + 2 * h, near),
+        )
+
+    to_near, to_far, relay = hops(
+        (near_send, near_recv), (far_send, far_recv), (relay_send, relay_recv), raw
+    )
+    if early:
+        (theirs, their_gate, their_up, their_down, scalars, their_scalars, *sems) = partner
+        slot_sems, near_sems, far_sems, relay_sems, weight_sems, scalar_sems = (
+            sems[i : i + 2] for i in range(0, 12, 2)
+        )
+
+        def to_peer(kind, h):
+            return remote(
+                raw.at[kind, h],
+                theirs.at[kind, h],
+                slot_sems[0].at[kind, h],
+                slot_sems[1].at[kind, h],
+                peer,
+            )
+
+        their_near, their_far, their_relay = hops(near_sems, far_sems, relay_sems, theirs)
+        first = pl.ds(0, CHUNK)
+        weight_copies = [
+            remote(src, dst, weight_sems[0].at[k], weight_sems[1].at[k], peer)
+            for k, (src, dst) in enumerate(
+                (
+                    (w_gate.at[:, first], their_gate),
+                    (w_up.at[:, first], their_up),
+                    (w_down.at[first], their_down),
+                )
+            )
+        ]
+        scalar_copy = remote(
+            scalars, their_scalars, scalar_sems[0].at[0], scalar_sems[1].at[0], peer
         )
 
     both = [(kind, h) for h in range(2) for kind in range(2)]
     for copy, (kind, h) in zip(slot_loads, both):
         copy.wait()
         to_far(kind, h).start()
+        if early:
+            to_peer(kind, h).start()
     for kind, h in both:
         to_near(kind, h).start()
     for copy in other_loads:
         copy.wait()
+    if early:
+        for copy in weight_copies:
+            copy.start()
 
     decay = 250.0 / (250.0 + jnp.full((8, 128), round_ref[0], jnp.int32).astype(jnp.float32))
     step = jnp.max(rate_ref[0] * decay)
-
-    def prepare(block):
+    count = count_ref[0].astype(jnp.float32)
+    if early:
+        scalars[0] = rate_ref[0] * decay
+        scalars[1] = jnp.full((8, 128), count, jnp.float32)
+
+    def prepare(blocks, block, count):
         to = pl.ds(pl.multiple_of(block * BLOCK, BLOCK), BLOCK)
-        floats = raw[0, block].astype(jnp.float32)
+        floats = blocks[0, block].astype(jnp.float32)
         scale = lax.rsqrt(jnp.mean(floats * floats, -1, keepdims=True) + 1e-06)
         value = (floats * scale).astype(jnp.bfloat16)
         normed[to] = value
         normed_t[:, to] = value.T
         slot = lax.bitwise_xor(shard, jnp.where(block < 4, block // 2, 2 + lax.rem(block, 2)))
-        live = jnp.where(slot < count_ref[0], 1.0, 0.0)
-        grad_out[to] = (raw[1, block].astype(jnp.float32) * live).astype(jnp.bfloat16)
+        live = jnp.where(slot.astype(jnp.float32) < count, 1.0, 0.0)
+        grad_out[to] = (blocks[1, block].astype(jnp.float32) * live).astype(jnp.bfloat16)
 
     def units_of(c):
         return pl.ds(pl.multiple_of(c * CHUNK, CHUNK), CHUNK)
 
-    def forward(c, block):
-        units = units_of(c)
+    def forward(gate_weight, up_weight, down_weight, block):
         at = pl.ds(pl.multiple_of(block * BLOCK, BLOCK), BLOCK)
         n = normed[at]
-        gate = jnp.dot(n, w_gate[:, units], preferred_element_type=jnp.float32)
-        up = jnp.dot(n, w_up[:, units], preferred_element_type=jnp.float32)
+        gate = jnp.dot(n, gate_weight[...], preferred_element_type=jnp.float32)
+        up = jnp.dot(n, up_weight[...], preferred_element_type=jnp.float32)
         back = lax.dot_general(
             grad_out[at],
-            w_down[units],
+            down_weight[...],
             (((1,), (1,)), ((), ())),
             preferred_element_type=jnp.float32,
         )
@@ -169,6 +213,10 @@
         d_both[at, :CHUNK] = (back * up * slope).astype(jnp.bfloat16)
         d_both[at, CHUNK:] = (back * act).astype(jnp.bfloat16)
 
+    def own_weights(c):
+        units = units_of(c)
+        return w_gate.at[:, units], w_up.at[:, units], w_down.at[units]
+
     @pl.loop(0, n_blocks)
     def _(block):
         @pl.when(block == 2)
@@ -189,8 +237,15 @@
             for kind in range(2):
                 relay(kind, h).wait_recv()
 
-        prepare(block)
-        forward(0, block)
+        prepare(raw, block, count)
+        forward(*own_weights(0), block)
+
+    if early:
+        scalar_copy.start()
+        for kind, h in both:
+            to_peer(kind, h).wait_recv()
+            their_far(kind, h).start()
+            their_near(kind, h).start()
 
     part = width // PARTS
     pairs = ((own_gate, got_gate), (own_up, got_up), (own_down, got_down))
@@ -199,22 +254,22 @@
         mine, theirs = (ref.at[c] if at is None else ref.at[c, at] for ref in pairs[k])
         return remote(mine, theirs, chunk_send.at[k, c], chunk_recv.at[k, c], peer)
 
-    @pl.loop(0, n_chunks)
-    def _(c):
-        units = units_of(c)
+    def update(weights, results, step, ready):
+        gate_weight, up_weight, down_weight = weights
+        gate_result, up_result, down_result = results
 
         @pl.loop(0, PARTS)
         def _(b):
             at = pl.ds(pl.multiple_of(b * part, part), part)
             grad = jnp.dot(normed_t[at], d_both[...], preferred_element_type=jnp.float32)
-            own_gate[c, at] = (
-                w_gate[at, units].astype(jnp.float32) - step * grad[:, :CHUNK]
+            gate_result[at] = (
+                gate_weight[at].astype(jnp.float32) - step * grad[:, :CHUNK]
             ).astype(jnp.bfloat16)
-            own_up[c, at] = (
-                w_up[at, units].astype(jnp.float32) - step * grad[:, CHUNK:]
+            up_result[at] = (
+                up_weight[at].astype(jnp.float32) - step * grad[:, CHUNK:]
             ).astype(jnp.bfloat16)
-            sent(0, c, at).start()
-            sent(1, c, at).start()
+            ready(0, at)
+            ready(1, at)
 
         hidden_t = hidden[...].T
 
@@ -222,17 +277,58 @@
         def _(b):
             at = pl.ds(pl.multiple_of(b * part, part), part)
             grad = jnp.dot(hidden_t, grad_out[:, at], preferred_element_type=jnp.float32)
-            own_down[c, :, at] = (
-                w_down[units, at].astype(jnp.float32) - step * grad
+            down_result[:, at] = (
+                down_weight[:, at].astype(jnp.float32) - step * grad
             ).astype(jnp.bfloat16)
 
-        sent(2, c).start()
+        ready(2, None)
+
+    @pl.loop(0, n_chunks)
+    def _(c):
+        def send(k, at):
+            if early:
+
+                @pl.when(c > 0)
+                def _():
+                    sent(k, c, at).start()
+
+            else:
+                sent(k, c, at).start()
+
+        update(
+            own_weights(c), (own_gate.at[c], own_up.at[c], own_down.at[c]), step, send
+        )
 
         @pl.when(c < n_chunks - 1)
         def _():
             @pl.loop(0, n_blocks)
             def _(block):
-                forward(c + 1, block)
+                forward(*own_weights(c + 1), block)
+
+    if early:
+        for kind, h in both:
+            their_far(kind, h).wait_recv()
+            their_relay(kind, h).start()
+            their_near(kind, h).wait_recv()
+        for copy in weight_copies:
+            copy.wait_recv()
+        scalar_copy.wait_recv()
+        for kind, h in both:
+            their_relay(kind, h).wait_recv()
+        their_step = jnp.max(their_scalars[0])
+        their_count = jnp.max(their_scalars[1])
+
+        @pl.loop(0, n_blocks)
+        def _(block):
+            prepare(theirs, block, their_count)
+            forward(their_gate, their_up, their_down, block)
+
+        update(
+            (their_gate, their_up, their_down),
+            (got_gate.at[0], got_up.at[0], got_down.at[0]),
+            their_step,
+            lambda k, at: None,
+        )
 
     def average(mine, theirs):
         return (0.5 * (mine.astype(jnp.float32) + theirs.astype(jnp.float32))).astype(jnp.bfloat16)
@@ -240,25 +336,40 @@
     @pl.loop(0, n_chunks)
     def _(c):
         units = units_of(c)
-        sent(0, c).wait_recv()
+
+        def arrived(k):
+            if early:
+
+                @pl.when(c > 0)
+                def _():
+                    sent(k, c).wait_recv()
+
+            else:
+                sent(k, c).wait_recv()
+
+        arrived(0)
         mixed_gate[:, units] = average(own_gate[c], got_gate[c])
-        sent(1, c).wait_recv()
+        arrived(1)
         mixed_up[:, units] = average(own_up[c], got_up[c])
-        sent(2, c).wait_recv()
+        arrived(2)
         mixed_down[units] = average(own_down[c], got_down[c])
 
-    @pl.loop(0, n_chunks)
+    @pl.loop(1 if early else 0, n_chunks)
     def _(c):
         for k in range(3):
             sent(k, c).wait_send()
 
+    gathers = [to_far, to_near, relay]
+    if early:
+        gathers += [to_peer, their_far, their_near, their_relay]
+        for copy in weight_copies + [scalar_copy]:
+            copy.wait_send()
     for kind, h in both:
-        to_far(kind, h).wait_send()
-        to_near(kind, h).wait_send()
-        relay(kind, h).wait_send()
-
-
-def one_level(level, count, round_index, rate, x, g, w_gate, w_up, w_down):
+        for copy in gathers:
+            copy(kind, h).wait_send()
+
+
+def one_level(level, early, count, round_index, rate, x, g, w_gate, w_up, w_down):
     seq, width = x.shape
     units = w_gate.shape[1]
     n_chunks, rows = units // CHUNK, 4 * seq
@@ -268,13 +379,23 @@
     dma = pltpu.SemaphoreType.DMA
     across = pltpu.VMEM((n_chunks, width, CHUNK), bf16)
     along = pltpu.VMEM((n_chunks, CHUNK, width), bf16)
+    raw = pltpu.VMEM((2, rows // BLOCK, BLOCK, width), bf16)
+    partner = [
+        raw,
+        pltpu.VMEM((width, CHUNK), bf16),
+        pltpu.VMEM((width, CHUNK), bf16),
+        pltpu.VMEM((CHUNK, width), bf16),
+        pltpu.VMEM((2, 8, 128), jnp.float32),
+        pltpu.VMEM((2, 8, 128), jnp.float32),
+    ]
+    partner += [dma((2, 2))] * 8 + [dma((3,))] * 2 + [dma((1,))] * 2
     mixed = pl.pallas_call(
-        functools.partial(round_kernel, level),
+        functools.partial(round_kernel, level, early),
         out_shape=[pltpu.VMEM(w.shape, bf16) for w in (w_gate, w_up, w_down)],
         in_specs=[hbm] * 8,
         out_specs=[vmem] * 3,
         scratch_shapes=[
-            pltpu.VMEM((2, rows // BLOCK, BLOCK, width), bf16),
+            raw,
             pltpu.VMEM((rows, width), bf16),
             pltpu.VMEM((width, rows), bf16),
             pltpu.VMEM((rows, width), bf16),
@@ -301,6 +422,7 @@
             dma((2, 2)),
             dma((3, n_chunks)),
             dma((3, n_chunks)),
+            *(partner if early else ()),
         ],
         compiler_params=pltpu.CompilerParams(
             collective_id=level, has_side_effects=True, vmem_limit_bytes=44 << 20
@@ -342,7 +464,7 @@
     levels = lax.axis_size("node").bit_length() - 1
     mixed = lax.switch(
         lax.rem(round_index[0], levels),
-        [functools.partial(one_level, level) for level in range(levels)],
+        [functools.partial(one_level, level, level < levels - 1) for level in range(levels)],
         counts,
         round_index,
         rates,

time: 214 us -> 211 us (0.986)
  Pallas kernels: 213 us -> 209 us
    pallas_call x1, Pallas kernels: 210 us -> 205 us  [one_level(): pl.pallas_call(functools.partial(round_kernel, level, early), out_shape=[...]
where the time goes in v3:
time: 211 us; the launch traced here: 210 us
  Pallas kernels  209 us (99%)
    pallas_call x1, Pallas kernels, one_level(): pl.pallas_call(functools.partial(round_kernel, level, early), out_shape=[...  205 us

profile of v3, /device:TPU:1, one launch (start us, length us, event | category | flops | bytes accessed | tf_op | source)
XLA Modules:
  0.0 210.4 jit_solution(9742570911983275864)
XLA Ops:
  1.3 209.0 %conditional.1 = ((bf16[1152,1152]{1,0:T(8,128)(2,1)}, bf16[1152,1152]{1,0:T(8,128)(2,1)}, bf16[1152,1152]{1,0:T(8,128)(2,1)})) conditional(s32[]{:T(128)} %bitcast, (s32[1]{0:T(128)}, s32[1]{0:T(128)}, f32[1]{0:T(128)}, bf16[256,1152]{1,0:T(8,128)(2,1)}, bf16[256,1152]{1,0:T(8,128)(2,1)}, ...), branch_computations={%region_0.0_spmd.clone, %region_1.0_spmd.clone, %region_2.0_spmd.c... | conditional | flops 16307453952 | bytes 17104904 | solution.py:465
  1.5 205.2 %round_level_3.1 = (bf16[1152,1152]{1,0:T(8,128)(2,1)S(1)}, bf16[1152,1152]{1,0:T(8,128)(2,1)S(1)}, bf16[1152,1152]{1,0:T(8,128)(2,1)S(1)}) custom-call(s32[1]{0:T(128)} %get-tuple-element.212.count_hbm, s32[1]{0:T(128)} %get-tuple-element.213.round_hbm, f32[1]{0:T(128)} %get-tuple-element.214.rate_hbm, bf16[256,1152]{1,0:T(8,128)(2,1)} %get-tuple-element.215.x_hbm, ...), custom_call_target="tpu_custom_call" | custom-call | flops 16307453952 | bytes 17104896 | tf_op jit(solution)/shard_map/cond/branch_3_fun/round_level_3/pallas_call | solution.py:392
  206.7 3.3 %write_out.8 = (bf16[1152,1152]{1,0:T(8,128)(2,1)}, bf16[1152,1152]{1,0:T(8,128)(2,1)}, bf16[1152,1152]{1,0:T(8,128)(2,1)}) custom-call(bf16[1152,1152]{1,0:T(8,128)(2,1)S(1)} %get-tuple-element.220.gate, bf16[1152,1152]{1,0:T(8,128)(2,1)S(1)} %get-tuple-element.221.up, bf16[1152,1152]{1,0:T(8,128)(2,1)S(1)} %get-tuple-element.222.down), custom_call_target="tpu_custom_call" | custom-call | tf_op jit(solution)/shard_map/cond/branch_3_fun/write_out/pallas_call | solution.py:452

commit v4 on v3

--- a/solution.py
+++ b/solution.py
@@ -127,17 +127,22 @@
         (near_send, near_recv), (far_send, far_recv), (relay_send, relay_recv), raw
     )
     if early:
-        (theirs, their_gate, their_up, their_down, scalars, their_scalars, *sems) = partner
-        slot_sems, near_sems, far_sems, relay_sems, weight_sems, scalar_sems = (
-            sems[i : i + 2] for i in range(0, 12, 2)
+        (theirs, their_gate, their_up, back_sent, their_back, scalars, their_scalars, *sems) = partner
+        slot_sems, near_sems, far_sems, relay_sems, weight_sems, back_sems, scalar_sems = (
+            sems[i : i + 2] for i in range(0, 14, 2)
         )
 
-        def to_peer(kind, h):
+        def to_peer(h):
             return remote(
-                raw.at[kind, h],
-                theirs.at[kind, h],
-                slot_sems[0].at[kind, h],
-                slot_sems[1].at[kind, h],
+                raw.at[0, h], theirs.at[0, h], slot_sems[0].at[h], slot_sems[1].at[h], peer
+            )
+
+        def back_copy(block):
+            return remote(
+                back_sent.at[block],
+                their_back.at[block],
+                back_sems[0].at[block],
+                back_sems[1].at[block],
                 peer,
             )
 
@@ -146,11 +151,7 @@
         weight_copies = [
             remote(src, dst, weight_sems[0].at[k], weight_sems[1].at[k], peer)
             for k, (src, dst) in enumerate(
-                (
-                    (w_gate.at[:, first], their_gate),
-                    (w_up.at[:, first], their_up),
-                    (w_down.at[first], their_down),
-                )
+                ((w_gate.at[:, first], their_gate), (w_up.at[:, first], their_up))
             )
         ]
         scalar_copy = remote(
@@ -161,8 +162,8 @@
     for copy, (kind, h) in zip(slot_loads, both):
         copy.wait()
         to_far(kind, h).start()
-        if early:
-            to_peer(kind, h).start()
+        if early and kind == 0:
+            to_peer(h).start()
     for kind, h in both:
         to_near(kind, h).start()
     for copy in other_loads:
@@ -175,8 +176,7 @@
     step = jnp.max(rate_ref[0] * decay)
     count = count_ref[0].astype(jnp.float32)
     if early:
-        scalars[0] = rate_ref[0] * decay
-        scalars[1] = jnp.full((8, 128), count, jnp.float32)
+        scalars[...] = rate_ref[0] * decay
 
     def prepare(blocks, block, count):
         to = pl.ds(pl.multiple_of(block * BLOCK, BLOCK), BLOCK)
@@ -185,6 +185,8 @@
         value = (floats * scale).astype(jnp.bfloat16)
         normed[to] = value
         normed_t[:, to] = value.T
+        if count is None:
+            return
         slot = lax.bitwise_xor(shard, jnp.where(block < 4, block // 2, 2 + lax.rem(block, 2)))
         live = jnp.where(slot.astype(jnp.float32) < count, 1.0, 0.0)
         grad_out[to] = (blocks[1, block].astype(jnp.float32) * live).astype(jnp.bfloat16)
@@ -192,30 +194,42 @@
     def units_of(c):
         return pl.ds(pl.multiple_of(c * CHUNK, CHUNK), CHUNK)
 
-    def forward(gate_weight, up_weight, down_weight, block):
+    def forward(gate_weight, up_weight, block, back_of, outputs):
         at = pl.ds(pl.multiple_of(block * BLOCK, BLOCK), BLOCK)
         n = normed[at]
         gate = jnp.dot(n, gate_weight[...], preferred_element_type=jnp.float32)
         up = jnp.dot(n, up_weight[...], preferred_element_type=jnp.float32)
-        back = lax.dot_general(
-            grad_out[at],
-            down_weight[...],
-            (((1,), (1,)), ((), ())),
-            preferred_element_type=jnp.float32,
-        )
+        back = back_of(at)
         k = 0.7978845608028654
         square = gate * gate
         t = jnp.tanh(gate * (k + (k * 0.044715) * square))
         half = 0.5 + 0.5 * t
         act = gate * half
         slope = half + (0.5 * gate) * (1.0 - t * t) * (k + (3.0 * k * 0.044715) * square)
-        hidden[at] = (act * up).astype(jnp.bfloat16)
+        if outputs:
+            hidden[at] = (act * up).astype(jnp.bfloat16)
         d_both[at, :CHUNK] = (back * up * slope).astype(jnp.bfloat16)
         d_both[at, CHUNK:] = (back * act).astype(jnp.bfloat16)
 
     def own_weights(c):
         units = units_of(c)
         return w_gate.at[:, units], w_up.at[:, units], w_down.at[units]
+
+    def own_forward(c, block, keep_back=False):
+        gate_weight, up_weight, down_weight = own_weights(c)
+
+        def back_of(at):
+            back = lax.dot_general(
+                grad_out[at],
+                down_weight[...],
+                (((1,), (1,)), ((), ())),
+                preferred_element_type=jnp.float32,
+            )
+            if keep_back:
+                back_sent[block] = back.astype(jnp.bfloat16)
+            return back
+
+        forward(gate_weight, up_weight, block, back_of, True)
 
     @pl.loop(0, n_blocks)
     def _(block):
@@ -238,14 +252,16 @@
                 relay(kind, h).wait_recv()
 
         prepare(raw, block, count)
-        forward(*own_weights(0), block)
+        own_forward(0, block, keep_back=early)
+        if early:
+            back_copy(block).start()
 
     if early:
         scalar_copy.start()
-        for kind, h in both:
-            to_peer(kind, h).wait_recv()
-            their_far(kind, h).start()
-            their_near(kind, h).start()
+        for h in range(2):
+            to_peer(h).wait_recv()
+            their_far(0, h).start()
+            their_near(0, h).start()
 
     part = width // PARTS
     pairs = ((own_gate, got_gate), (own_up, got_up), (own_down, got_down))
@@ -254,9 +270,9 @@
         mine, theirs = (ref.at[c] if at is None else ref.at[c, at] for ref in pairs[k])
         return remote(mine, theirs, chunk_send.at[k, c], chunk_recv.at[k, c], peer)
 
-    def update(weights, results, step, ready):
-        gate_weight, up_weight, down_weight = weights
-        gate_result, up_result, down_result = results
+    def update_across(weights, results, step, ready):
+        gate_weight, up_weight = weights
+        gate_result, up_result = results
 
         @pl.loop(0, PARTS)
         def _(b):
@@ -268,66 +284,73 @@
             up_result[at] = (
                 up_weight[at].astype(jnp.float32) - step * grad[:, CHUNK:]
             ).astype(jnp.bfloat16)
-            ready(0, at)
-            ready(1, at)
-
+            ready(at)
+
+    def update_down(weight, result):
         hidden_t = hidden[...].T
 
         @pl.loop(0, PARTS)
         def _(b):
             at = pl.ds(pl.multiple_of(b * part, part), part)
             grad = jnp.dot(hidden_t, grad_out[:, at], preferred_element_type=jnp.float32)
-            down_result[:, at] = (
-                down_weight[:, at].astype(jnp.float32) - step * grad
-            ).astype(jnp.bfloat16)
-
-        ready(2, None)
+            result[:, at] = (weight[:, at].astype(jnp.float32) - step * grad).astype(jnp.bfloat16)
+
+    def across_travels(c, act):
+        if early:
+            pl.when(c > 0)(act)
+        else:
+            act()
 
     @pl.loop(0, n_chunks)
     def _(c):
-        def send(k, at):
-            if early:
-
-                @pl.when(c > 0)
-                def _():
-                    sent(k, c, at).start()
-
-            else:
-                sent(k, c, at).start()
-
-        update(
-            own_weights(c), (own_gate.at[c], own_up.at[c], own_down.at[c]), step, send
-        )
+        weights = own_weights(c)
+
+        def send(at):
+            def start():
+                sent(0, c, at).start()
+                sent(1, c, at).start()
+
+            across_travels(c, start)
+
+        def down():
+            update_down(weights[2], own_down.at[c])
+            sent(2, c).start()
+
+        update_across(weights[:2], (own_gate.at[c], own_up.at[c]), step, send)
+        down()
 
         @pl.when(c < n_chunks - 1)
         def _():
             @pl.loop(0, n_blocks)
             def _(block):
-                forward(*own_weights(c + 1), block)
+                own_forward(c + 1, block)
 
     if early:
-        for kind, h in both:
-            their_far(kind, h).wait_recv()
-            their_relay(kind, h).start()
-            their_near(kind, h).wait_recv()
+        for h in range(2):
+            their_far(0, h).wait_recv()
+            their_relay(0, h).start()
+            their_near(0, h).wait_recv()
         for copy in weight_copies:
             copy.wait_recv()
         scalar_copy.wait_recv()
-        for kind, h in both:
-            their_relay(kind, h).wait_recv()
-        their_step = jnp.max(their_scalars[0])
-        their_count = jnp.max(their_scalars[1])
+        for h in range(2):
+            their_relay(0, h).wait_recv()
+        their_step = jnp.max(their_scalars[...])
 
         @pl.loop(0, n_blocks)
         def _(block):
-            prepare(theirs, block, their_count)
-            forward(their_gate, their_up, their_down, block)
-
-        update(
-            (their_gate, their_up, their_down),
-            (got_gate.at[0], got_up.at[0], got_down.at[0]),
-            their_step,
-            lambda k, at: None,
+            prepare(theirs, block, None)
+            back_copy(block).wait_recv()
+            forward(
+                their_gate,
+                their_up,
+                block,
+                lambda at: their_back[block].astype(jnp.float32),
+                False,
+            )
+
+        update_across(
+            (their_gate, their_up), (got_gate.at[0], got_up.at[0]), their_step, lambda at: None
         )
 
     def average(mine, theirs):
@@ -337,36 +360,33 @@
     def _(c):
         units = units_of(c)
 
-        def arrived(k):
-            if early:
-
-                @pl.when(c > 0)
-                def _():
-                    sent(k, c).wait_recv()
-
-            else:
-                sent(k, c).wait_recv()
-
-        arrived(0)
+        across_travels(c, lambda: sent(0, c).wait_recv())
         mixed_gate[:, units] = average(own_gate[c], got_gate[c])
-        arrived(1)
+        across_travels(c, lambda: sent(1, c).wait_recv())
         mixed_up[:, units] = average(own_up[c], got_up[c])
-        arrived(2)
+        sent(2, c).wait_recv()
         mixed_down[units] = average(own_down[c], got_down[c])
 
-    @pl.loop(1 if early else 0, n_chunks)
+    @pl.loop(0, n_chunks)
     def _(c):
-        for k in range(3):
-            sent(k, c).wait_send()
-
-    gathers = [to_far, to_near, relay]
+        across_travels(c, lambda: sent(0, c).wait_send())
+        across_travels(c, lambda: sent(1, c).wait_send())
+        sent(2, c).wait_send()
+
+    for kind, h in both:
+        for copy in (to_far, to_near, relay):
+            copy(kind, h).wait_send()
     if early:
-        gathers += [to_peer, their_far, their_near, their_relay]
         for copy in weight_copies + [scalar_copy]:
             copy.wait_send()
-    for kind, h in both:
-        for copy in gathers:
-            copy(kind, h).wait_send()
+        for h in range(2):
+            to_peer(h).wait_send()
+            for copy in (their_far, their_near, their_relay):
+                copy(0, h).wait_send()
+
+        @pl.loop(0, n_blocks)
+        def _(block):
+            back_copy(block).wait_send()
 
 
 def one_level(level, early, count, round_index, rate, x, g, w_gate, w_up, w_down):
@@ -380,15 +400,13 @@
     across = pltpu.VMEM((n_chunks, width, CHUNK), bf16)
     along = pltpu.VMEM((n_chunks, CHUNK, width), bf16)
     raw = pltpu.VMEM((2, rows // BLOCK, BLOCK, width), bf16)
-    partner = [
-        raw,
-        pltpu.VMEM((width, CHUNK), bf16),
-        pltpu.VMEM((width, CHUNK), bf16),
-        pltpu.VMEM((CHUNK, width), bf16),
-        pltpu.VMEM((2, 8, 128), jnp.float32),
-        pltpu.VMEM((2, 8, 128), jnp.float32),
-    ]
-    partner += [dma((2, 2))] * 8 + [dma((3,))] * 2 + [dma((1,))] * 2
+    column = pltpu.VMEM((width, CHUNK), bf16)
+    backs = pltpu.VMEM((rows // BLOCK, BLOCK, CHUNK), bf16)
+    scalar = pltpu.VMEM((8, 128), jnp.float32)
+    partner = [pltpu.VMEM((1, rows // BLOCK, BLOCK, width), bf16)]
+    partner += [column, column, backs, backs, scalar, scalar]
+    partner += [dma((2,))] * 2 + [dma((1, 2))] * 6 + [dma((2,))] * 2
+    partner += [dma((rows // BLOCK,))] * 2 + [dma((1,))] * 2
     mixed = pl.pallas_call(
         functools.partial(round_kernel, level, early),
         out_shape=[pltpu.VMEM(w.shape, bf16) for w in (w_gate, w_up, w_down)],

time: 211 us -> 205 us (0.972)
  Pallas kernels: 209 us -> 203 us
    pallas_call x1, Pallas kernels: 205 us -> 199 us  [one_level(): pl.pallas_call(functools.partial(round_kernel, level, early), out_shape=[...]
where the time goes in v4:
time: 205 us; the launch traced here: 204 us
  Pallas kernels  203 us (99%)
    pallas_call x1, Pallas kernels, one_level(): pl.pallas_call(functools.partial(round_kernel, level, early), out_shape=[...  199 us

profile of v4, /device:TPU:1, one launch (start us, length us, event | category | flops | bytes accessed | tf_op | source)
XLA Modules:
  0.0 204.5 jit_solution(10186010726436674648)
XLA Ops:
  1.3 203.0 %conditional.1 = ((bf16[1152,1152]{1,0:T(8,128)(2,1)}, bf16[1152,1152]{1,0:T(8,128)(2,1)}, bf16[1152,1152]{1,0:T(8,128)(2,1)})) conditional(s32[]{:T(128)} %bitcast, (s32[1]{0:T(128)}, s32[1]{0:T(128)}, f32[1]{0:T(128)}, bf16[256,1152]{1,0:T(8,128)(2,1)}, bf16[256,1152]{1,0:T(8,128)(2,1)}, ...), branch_computations={%region_0.0_spmd.clone, %region_1.0_spmd.clone, %region_2.0_spmd.c... | conditional | flops 16307453952 | bytes 17104904 | solution.py:483
  1.5 199.3 %round_level_3.1 = (bf16[1152,1152]{1,0:T(8,128)(2,1)S(1)}, bf16[1152,1152]{1,0:T(8,128)(2,1)S(1)}, bf16[1152,1152]{1,0:T(8,128)(2,1)S(1)}) custom-call(s32[1]{0:T(128)} %get-tuple-element.212.count_hbm, s32[1]{0:T(128)} %get-tuple-element.213.round_hbm, f32[1]{0:T(128)} %get-tuple-element.214.rate_hbm, bf16[256,1152]{1,0:T(8,128)(2,1)} %get-tuple-element.215.x_hbm, ...), custom_call_target="tpu_custom_call" | custom-call | flops 16307453952 | bytes 17104896 | tf_op jit(solution)/shard_map/cond/branch_3_fun/round_level_3/pallas_call | solution.py:410
  200.8 3.3 %write_out.8 = (bf16[1152,1152]{1,0:T(8,128)(2,1)}, bf16[1152,1152]{1,0:T(8,128)(2,1)}, bf16[1152,1152]{1,0:T(8,128)(2,1)}) custom-call(bf16[1152,1152]{1,0:T(8,128)(2,1)S(1)} %get-tuple-element.220.gate, bf16[1152,1152]{1,0:T(8,128)(2,1)S(1)} %get-tuple-element.221.up, bf16[1152,1152]{1,0:T(8,128)(2,1)S(1)} %get-tuple-element.222.down), custom_call_target="tpu_custom_call" | custom-call | tf_op jit(solution)/shard_map/cond/branch_3_fun/write_out/pallas_call | solution.py:470

commit v5 on v2

v5 whole, which is shorter than its diff:
```python
import functools

import jax
import jax.numpy as jnp
from jax import lax
from jax.experimental import pallas as pl
from jax.experimental.pallas import tpu as pltpu
from jax.sharding import PartitionSpec as P

MESH = pl.DeviceIdType.MESH
CHUNK = 128
BLOCK = 128
PIECE = 64
PARTS = 3

EARLY = ((0, 0, 5), (1, 0, 6), (0, 1, 7))
FIRST_LATE = min(blocks for _, _, blocks in EARLY)


def remote(src, dst, send_sem, recv_sem, device):
    return pltpu.make_async_remote_copy(
        src_ref=src,
        dst_ref=dst,
        send_sem=send_sem,
        recv_sem=recv_sem,
        device_id=device,
        device_id_type=MESH,
    )


def round_kernel(
    level,
    early,
    count_hbm,
    round_hbm,
    rate_hbm,
    x_hbm,
    g_hbm,
    wg_hbm,
    wu_hbm,
    wd_hbm,
    mixed_gate,
    mixed_up,
    mixed_down,
    raw,
    normed,
    normed_t,
    grad_out,
    w_gate,
    w_up,
    w_down,
    d_both,
    hidden,
    own_gate,
    own_up,
    own_down,
    got_gate,
    got_up,
    got_down,
    count_ref,
    round_ref,
    rate_ref,
    local_sem,
    near_send,
    near_recv,
    far_send,
    far_recv,
    relay_send,
    relay_recv,
    chunk_send,
    chunk_recv,
    *partner,
):
    node, shard = lax.axis_index("node"), lax.axis_index("shard")
    core, chip = lax.rem(shard, 2), shard // 2
    near = (node, chip * 2 + 1 - core)
    far = (node, (1 - chip) * 2 + core)
    stride = 1 << level
    peer = (node + (1 - 2 * lax.rem(node // stride, 2)) * stride, shard)
    n_blocks = raw.shape[1]
    width = normed.shape[1]
    n_chunks = own_gate.shape[0]

    def load(i, src, dst):
        return pltpu.make_async_copy(src, dst, local_sem.at[i])

    def rows_of(h):
        return pl.ds(h * BLOCK, BLOCK)

    slot_loads = [
        load(kind * 2 + h, src.at[rows_of(h)], raw.at[kind, h])
        for h in range(2)
        for kind, src in enumerate((x_hbm, g_hbm))
    ]
    other_loads = [
        load(4, wg_hbm, w_gate),
        load(5, wu_hbm, w_up),
        load(6, wd_hbm, w_down),
        load(7, count_hbm, count_ref),
        load(8, round_hbm, round_ref),
        load(9, rate_hbm, rate_ref),
    ]
    for copy in slot_loads:
        copy.start()

    barrier = pltpu.get_barrier_semaphore()
    for device in (near, far, peer):
        pl.semaphore_signal(barrier, inc=1, device_id=device, device_id_type=MESH)
    pl.semaphore_wait(barrier, 3)

    n_pieces = n_blocks - 4
    per_block = BLOCK // PIECE
    head, tail = pl.ds(0, PIECE), pl.ds(PIECE, PIECE)

    def own_piece(kind, i):
        start = pl.multiple_of((i % per_block) * PIECE, PIECE)
        return raw.at[kind, i // per_block, pl.ds(start, PIECE)]

    def to_near(kind, h):
        return remote(
            raw.at[kind, h], raw.at[kind, 2 + h], near_send.at[kind, h], near_recv.at[kind, h], near
        )

    def to_far(kind, i):
        return remote(
            own_piece(kind, i),
            raw.at[kind, 4 + i, head],
            far_send.at[kind, i],
            far_recv.at[kind, i],
            far,
        )

    def relay(kind, i):
        return remote(
            raw.at[kind, 4 + i, head],
            raw.at[kind, 4 + i, tail],
            relay_send.at[kind, i],
            relay_recv.at[kind, i],
            near,
        )

    both = [(kind, h) for h in range(2) for kind in range(2)]
    pieces = [(kind, i) for i in range(n_pieces) for kind in range(2)]
    pairs = ((own_gate, got_gate), (own_up, got_up), (own_down, got_down))
    if early:
        (passing, theirs, partial, late, their_late, scalars, their_scalars, *sems) = partner
        slot_sems, far_sems, relay_sems, late_sems, scalar_sems = (
            sems[i : i + 2] for i in range(0, 10, 2)
        )
        skipped = FIRST_LATE - 4
        late_blocks = range(skipped, n_pieces)

        def to_peer(j):
            return remote(
                own_piece(0, j + skipped),
                passing.at[j],
                slot_sems[0].at[j],
                slot_sems[1].at[j],
                peer,
            )

        def their_far(j):
            return remote(
                passing.at[j], theirs.at[0, j, head], far_sems[0].at[j], far_sems[1].at[j], far
            )

        def their_relay(j):
            return remote(
                theirs.at[0, j, head],
                theirs.at[0, j, tail],
                relay_sems[0].at[j],
                relay_sems[1].at[j],
                near,
            )

        def late_copy(item, j):
            rows = pl.ds(pl.multiple_of(j * BLOCK, BLOCK), BLOCK)
            return remote(
                late.at[item, rows],
                their_late.at[item, rows],
                late_sems[0].at[item, j],
                late_sems[1].at[item, j],
                peer,
            )

        def early_copy(item, at=None):
            k, c, _ = EARLY[item]
            mine, other = partial.at[item], pairs[k][1].at[c]
            if at is not None:
                mine, other = mine.at[at], other.at[at]
            return remote(mine, other, chunk_send.at[k, c], chunk_recv.at[k, c], peer)

        scalar_copy = remote(
            scalars, their_scalars, scalar_sems[0].at[0], scalar_sems[1].at[0], peer
        )

    for h in range(2):
        for kind in range(2):
            slot_loads[2 * h + kind].wait()
        for i in range(h * per_block, (h + 1) * per_block):
            for kind in range(2):
                to_far(kind, i).start()
            if early and i >= skipped:
                to_peer(i - skipped).start()
    for copy in other_loads:
        copy.start()
    for kind, h in both:
        to_near(kind, h).start()
    for copy in other_loads:
        copy.wait()

    decay = 250.0 / (250.0 + jnp.full((8, 128), round_ref[0], jnp.int32).astype(jnp.float32))
    step = jnp.max(rate_ref[0] * decay)
    count = count_ref[0].astype(jnp.float32)
    if early:
        scalars[...] = rate_ref[0] * decay

    def prepare(blocks, block, count):
        to = pl.ds(pl.multiple_of(block * BLOCK, BLOCK), BLOCK)
        floats = blocks[0, block].astype(jnp.float32)
        scale = lax.rsqrt(jnp.mean(floats * floats, -1, keepdims=True) + 1e-06)
        value = (floats * scale).astype(jnp.bfloat16)
        normed[to] = value
        normed_t[:, to] = value.T
        if count is None:
            return
        for half, rest in ((0, 2), (1, 3)):
            slot = lax.bitwise_xor(shard, jnp.where(block < 4, block // 2, rest))
            live = jnp.where(slot.astype(jnp.float32) < count, 1.0, 0.0)
            start = pl.multiple_of(block * BLOCK + half * PIECE, PIECE)
            grad_out[pl.ds(start, PIECE)] = (
                blocks[1, block, half * PIECE : (half + 1) * PIECE].astype(jnp.float32) * live
            ).astype(jnp.bfloat16)

    def units_of(c):
        return pl.ds(pl.multiple_of(c * CHUNK, CHUNK), CHUNK)

    def own_weights(c):
        units = units_of(c)
        return w_gate.at[:, units], w_up.at[:, units], w_down.at[units]

    def forward(c, block):
        gate_weight, up_weight, down_weight = own_weights(c)
        buffer = lax.rem(c, 2)
        at = pl.ds(pl.multiple_of(block * BLOCK, BLOCK), BLOCK)
        n = normed[at]
        gate = jnp.dot(n, gate_weight[...], preferred_element_type=jnp.float32)
        up = jnp.dot(n, up_weight[...], preferred_element_type=jnp.float32)
        back = lax.dot_general(
            grad_out[at],
            down_weight[...],
            (((1,), (1,)), ((), ())),
            preferred_element_type=jnp.float32,
        )
        k = 0.7978845608028654
        square = gate * gate
        t = jnp.tanh(gate * (k + (k * 0.044715) * square))
        half = 0.5 + 0.5 * t
        act = gate * half
        slope = half + (0.5 * gate) * (1.0 - t * t) * (k + (3.0 * k * 0.044715) * square)
        hidden[buffer, at] = (act * up).astype(jnp.bfloat16)
        d_both[buffer, at, :CHUNK] = (back * up * slope).astype(jnp.bfloat16)
        d_both[buffer, at, CHUNK:] = (back * act).astype(jnp.bfloat16)

    part = width // PARTS

    def part_of(b):
        return pl.ds(pl.multiple_of(b * part, part), part)

    def send_early(item):
        k, c, blocks = EARLY[item]
        weight = own_weights(c)[k]
        rows = blocks * BLOCK

        @pl.loop(0, PARTS)
        def _(b):
            at = part_of(b)
            grad = jnp.dot(
                normed_t[at, :rows],
                d_both[c, :rows, k * CHUNK : (k + 1) * CHUNK],
                preferred_element_type=jnp.float32,
            )
            partial[item, at] = (weight[at].astype(jnp.float32) - step * grad).astype(
                jnp.bfloat16
            )
            early_copy(item, at).start()

    def send_late(item, block):
        k, c, _ = EARLY[item]
        at = pl.ds(pl.multiple_of(block * BLOCK, BLOCK), BLOCK)
        to = pl.ds(pl.multiple_of((block - FIRST_LATE) * BLOCK, BLOCK), BLOCK)
        late[item, to] = d_both[c, at, k * CHUNK : (k + 1) * CHUNK]
        late_copy(item, block - FIRST_LATE).start()

    ahead = 2 if early else 1

    @pl.loop(0, n_blocks)
    def _(block):
        @pl.when(block == 2)
        def _():
            for kind, h in both:
                to_near(kind, h).wait_recv()

        @pl.when(block >= 4)
        def _():
            for kind in range(2):
                to_far(kind, block - 4).wait_recv()
                relay(kind, block - 4).start()
            for kind in range(2):
                relay(kind, block - 4).wait_recv()

        prepare(raw, block, count)
        for c in range(ahead):
            forward(c, block)
        if early:
            for item, (_, _, blocks) in enumerate(EARLY):
                pl.when(block >= blocks)(functools.partial(send_late, item, block))
            for item, (_, _, blocks) in enumerate(EARLY):
                pl.when(block == blocks - 1)(functools.partial(send_early, item))

    if early:
        scalar_copy.start()
        for j in range(len(late_blocks)):
            to_peer(j).wait_recv()
            their_far(j).start()

    def sent(k, c, at=None):
        mine, other = (ref.at[c] if at is None else ref.at[c, at] for ref in pairs[k])
        return remote(mine, other, chunk_send.at[k, c], chunk_recv.at[k, c], peer)

    def if_late(k, c, act):
        chunks = [chunk for matrix, chunk, _ in EARLY if matrix == k] if early else []
        if chunks:
            pl.when(c > max(chunks))(act)
        else:
            act()

    @pl.loop(0, n_chunks)
    def _(c):
        gate_weight, up_weight, down_weight = own_weights(c)
        buffer = lax.rem(c, 2)

        hidden_t = hidden[buffer].T

        @pl.loop(0, PARTS)
        def _(b):
            at = part_of(b)
            grad = jnp.dot(normed_t[at], d_both[buffer], preferred_element_type=jnp.float32)
            own_gate[c, at] = (
                gate_weight[at].astype(jnp.float32) - step * grad[:, :CHUNK]
            ).astype(jnp.bfloat16)
            own_up[c, at] = (
                up_weight[at].astype(jnp.float32) - step * grad[:, CHUNK:]
            ).astype(jnp.bfloat16)
            for k in range(2):
                if_late(k, c, lambda: sent(k, c, at).start())

        @pl.loop(0, PARTS)
        def _(b):
            at = part_of(b)
            grad = jnp.dot(hidden_t, grad_out[:, at], preferred_element_type=jnp.float32)
            own_down[c, :, at] = (
                down_weight[:, at].astype(jnp.float32) - step * grad
            ).astype(jnp.bfloat16)

        sent(2, c).start()

        @pl.when(c < n_chunks - ahead)
        def _():
            @pl.loop(0, n_blocks)
            def _(block):
                forward(c + ahead, block)

    if early:
        for j in range(len(late_blocks)):
            their_far(j).wait_recv()
            their_relay(j).start()
        for item, (_, _, blocks) in enumerate(EARLY):
            early_copy(item).wait_recv()
            for j in range(len(late_blocks)):
                if FIRST_LATE + j >= blocks:
                    late_copy(item, j).wait_recv()
                else:
                    their_late[item, j * BLOCK : (j + 1) * BLOCK] = jnp.zeros(
                        (BLOCK, CHUNK), jnp.bfloat16
                    )
        scalar_copy.wait_recv()
        for j in range(len(late_blocks)):
            their_relay(j).wait_recv()
        their_step = jnp.max(their_scalars[...])

        @pl.loop(0, len(late_blocks))
        def _(j):
            prepare(theirs, j, None)

        for item, (k, c, _) in enumerate(EARLY):
            result = pairs[k][1].at[c]

            @pl.loop(0, PARTS)
            def _(b):
                at = part_of(b)
                grad = jnp.dot(
                    normed_t[at, : len(late_blocks) * BLOCK],
                    their_late[item],
                    preferred_element_type=jnp.float32,
                )
                result[at] = (result[at].astype(jnp.float32) - their_step * grad).astype(
                    jnp.bfloat16
                )

    def average(mine, theirs):
        return (0.5 * (mine.astype(jnp.float32) + theirs.astype(jnp.float32))).astype(jnp.bfloat16)

    @pl.loop(0, n_chunks)
    def _(c):
        units = units_of(c)

        if_late(0, c, lambda: sent(0, c).wait_recv())
        mixed_gate[:, units] = average(own_gate[c], got_gate[c])
        if_late(1, c, lambda: sent(1, c).wait_recv())
        mixed_up[:, units] = average(own_up[c], got_up[c])
        sent(2, c).wait_recv()
        mixed_down[units] = average(own_down[c], got_down[c])

    @pl.loop(0, n_chunks)
    def _(c):
        if_late(0, c, lambda: sent(0, c).wait_send())
        if_late(1, c, lambda: sent(1, c).wait_send())
        sent(2, c).wait_send()

    for kind, h in both:
        to_near(kind, h).wait_send()
    for kind, i in pieces:
        to_far(kind, i).wait_send()
        relay(kind, i).wait_send()
    if early:
        scalar_copy.wait_send()
        for j in range(len(late_blocks)):
            to_peer(j).wait_send()
            their_far(j).wait_send()
            their_relay(j).wait_send()
        for item, (_, _, blocks) in enumerate(EARLY):
            early_copy(item).wait_send()
            for j in range(blocks - FIRST_LATE, len(late_blocks)):
                late_copy(item, j).wait_send()


def one_level(level, early, count, round_index, rate, x, g, w_gate, w_up, w_down):
    seq, width = x.shape
    units = w_gate.shape[1]
    n_chunks, rows = units // CHUNK, 4 * seq
    bf16 = jnp.bfloat16
    hbm = pl.BlockSpec(memory_space=pltpu.HBM)
    vmem = pl.BlockSpec(memory_space=pltpu.VMEM)
    dma = pltpu.SemaphoreType.DMA
    across = pltpu.VMEM((n_chunks, width, CHUNK), bf16)
    along = pltpu.VMEM((n_chunks, CHUNK, width), bf16)
    raw = pltpu.VMEM((2, rows // BLOCK, BLOCK, width), bf16)
    n_pieces = seq // PIECE
    n_late = 4 + n_pieces - FIRST_LATE
    late = pltpu.VMEM((len(EARLY), n_late * BLOCK, CHUNK), bf16)
    scalar = pltpu.VMEM((8, 128), jnp.float32)
    partner = [
        pltpu.VMEM((n_late, PIECE, width), bf16),
        pltpu.VMEM((1, n_late, BLOCK, width), bf16),
        pltpu.VMEM((len(EARLY), width, CHUNK), bf16),
        late,
        late,
        scalar,
        scalar,
    ]
    partner += [dma((n_late,))] * 6 + [dma((len(EARLY), n_late))] * 2 + [dma((1,))] * 2
    mixed = pl.pallas_call(
        functools.partial(round_kernel, level, early),
        out_shape=[pltpu.VMEM(w.shape, bf16) for w in (w_gate, w_up, w_down)],
        in_specs=[hbm] * 8,
        out_specs=[vmem] * 3,
        scratch_shapes=[
            raw,
            pltpu.VMEM((rows, width), bf16),
            pltpu.VMEM((width, rows), bf16),
            pltpu.VMEM((rows, width), bf16),
            pltpu.VMEM(w_gate.shape, bf16),
            pltpu.VMEM(w_up.shape, bf16),
            pltpu.VMEM(w_down.shape, bf16),
            pltpu.VMEM((2, rows, 2 * CHUNK), bf16),
            pltpu.VMEM((2, rows, CHUNK), bf16),
            across,
            across,
            along,
            across,
            across,
            along,
            pltpu.SMEM((1,), jnp.int32),
            pltpu.SMEM((1,), jnp.int32),
            pltpu.SMEM((1,), jnp.float32),
            dma((10,)),
            dma((2, 2)),
            dma((2, 2)),
            dma((2, n_pieces)),
            dma((2, n_pieces)),
            dma((2, n_pieces)),
            dma((2, n_pieces)),
            dma((3, n_chunks)),
            dma((3, n_chunks)),
            *(partner if early else ()),
        ],
        compiler_params=pltpu.CompilerParams(
            collective_id=level, has_side_effects=True, vmem_limit_bytes=44 << 20
        ),
        cost_estimate=pl.CostEstimate(
            flops=12 * rows * width * units,
            bytes_accessed=2 * (6 * width * units + 2 * seq * width),
            transcendentals=rows * units,
        ),
        name=f"round_level_{level}",
    )(count, round_index, rate, x, g, w_gate, w_up, w_down)
    return write_out(*mixed)


def write_kernel(gate, up, down, out_gate, out_up, out_down, sem):
    copies = [
        pltpu.make_async_copy(src, dst, sem.at[i])
        for i, (src, dst) in enumerate(((gate, out_gate), (up, out_up), (down, out_down)))
    ]
    for copy in copies:
        copy.start()
    for copy in copies:
        copy.wait()


def write_out(*arrays):
    return pl.pallas_call(
        write_kernel,
        out_shape=[jax.ShapeDtypeStruct(a.shape, a.dtype) for a in arrays],
        in_specs=[pl.BlockSpec(memory_space=pltpu.VMEM)] * 3,
        out_specs=[pl.BlockSpec(memory_space=pltpu.HBM)] * 3,
        scratch_shapes=[pltpu.SemaphoreType.DMA((3,))],
        compiler_params=pltpu.CompilerParams(vmem_limit_bytes=16 << 20),
        name="write_out",
    )(*arrays)


def per_device(inputs, upstream, counts, round_index, rates, gate_weight, up_weight, down_weight):
    levels = lax.axis_size("node").bit_length() - 1
    mixed = lax.switch(
        lax.rem(round_index[0], levels),
        [functools.partial(one_level, level, level < levels - 1) for level in range(levels)],
        counts,
        round_index,
        rates,
        inputs[0],
        upstream[0],
        gate_weight[0],
        up_weight[0],
        down_weight[0],
    )
    return tuple(m[None] for m in mixed)


def solution(mesh):
    return jax.shard_map(
        per_device,
        mesh=mesh,
        in_specs=(
            P("node", "shard", None),
            P("node", "shard", None),
            P("node"),
            P(),
            P("node"),
            P("node", None, "shard"),
            P("node", None, "shard"),
            P("node", "shard", None),
        ),
        out_specs=(P("node", None, "shard"), P("node", None, "shard"), P("node", "shard", None)),
        check_vma=False,
    )
```

time: 214 us -> 201 us (0.939)
  Pallas kernels: 213 us -> 199 us
    pallas_call x1, Pallas kernels: 210 us -> 196 us  [one_level(): pl.pallas_call(functools.partial(round_kernel, level, early), out_shape=[...]
where the time goes in v5:
time: 201 us
  Pallas kernels  199 us (99%)
    pallas_call x1, Pallas kernels, one_level(): pl.pallas_call(functools.partial(round_kernel, level, early), out_shape=[...  196 us

profile of v5, /device:TPU:1, one launch (start us, length us, event | category | flops | bytes accessed | tf_op | source)
XLA Modules:
  0.0 201.3 jit_solution(17663622020867491560)
XLA Ops:
  1.3 199.9 %conditional.1 = ((bf16[1152,1152]{1,0:T(8,128)(2,1)}, bf16[1152,1152]{1,0:T(8,128)(2,1)}, bf16[1152,1152]{1,0:T(8,128)(2,1)})) conditional(s32[]{:T(128)} %bitcast, (s32[1]{0:T(128)}, s32[1]{0:T(128)}, f32[1]{0:T(128)}, bf16[256,1152]{1,0:T(8,128)(2,1)}, bf16[256,1152]{1,0:T(8,128)(2,1)}, ...), branch_computations={%region_0.0_spmd.clone, %region_1.0_spmd.clone, %region_2.0_spmd.c... | conditional | flops 16307453952 | bytes 17104904 | solution.py:546
  1.5 196.1 %round_level_3.1 = (bf16[1152,1152]{1,0:T(8,128)(2,1)S(1)}, bf16[1152,1152]{1,0:T(8,128)(2,1)S(1)}, bf16[1152,1152]{1,0:T(8,128)(2,1)S(1)}) custom-call(s32[1]{0:T(128)} %get-tuple-element.212.count_hbm, s32[1]{0:T(128)} %get-tuple-element.213.round_hbm, f32[1]{0:T(128)} %get-tuple-element.214.rate_hbm, bf16[256,1152]{1,0:T(8,128)(2,1)} %get-tuple-element.215.x_hbm, ...), custom_call_target="tpu_custom_call" | custom-call | flops 16307453952 | bytes 17104896 | tf_op jit(solution)/shard_map/cond/branch_3_fun/round_level_3/pallas_call | solution.py:473
  197.6 3.3 %write_out.8 = (bf16[1152,1152]{1,0:T(8,128)(2,1)}, bf16[1152,1152]{1,0:T(8,128)(2,1)}, bf16[1152,1152]{1,0:T(8,128)(2,1)}) custom-call(bf16[1152,1152]{1,0:T(8,128)(2,1)S(1)} %get-tuple-element.220.gate, bf16[1152,1152]{1,0:T(8,128)(2,1)S(1)} %get-tuple-element.221.up, bf16[1152,1152]{1,0:T(8,128)(2,1)S(1)} %get-tuple-element.222.down), custom_call_target="tpu_custom_call" | custom-call | tf_op jit(solution)/shard_map/cond/branch_3_fun/write_out/pallas_call | solution.py:533

commit v6 on v5

--- a/solution.py
+++ b/solution.py
@@ -14,7 +14,11 @@
 PARTS = 3
 
 EARLY = ((0, 0, 5), (1, 0, 6), (0, 1, 7))
-FIRST_LATE = min(blocks for _, _, blocks in EARLY)
+EARLY_SHARED = ((0, 0, 7),)
+
+
+def first_late(early):
+    return min(blocks for _, _, blocks in early)
 
 
 def remote(src, dst, send_sem, recv_sem, device):
@@ -31,6 +35,7 @@
 def round_kernel(
     level,
     early,
+    direct,
     count_hbm,
     round_hbm,
     rate_hbm,
@@ -69,14 +74,31 @@
     relay_recv,
     chunk_send,
     chunk_recv,
-    *partner,
+    passing,
+    theirs,
+    partial,
+    late,
+    their_late,
+    scalars,
+    their_scalars,
+    slot_send,
+    slot_recv,
+    across_send,
+    across_recv,
+    pass_send,
+    pass_recv,
+    late_send,
+    late_recv,
+    scalar_send,
+    scalar_recv,
 ):
     node, shard = lax.axis_index("node"), lax.axis_index("shard")
     core, chip = lax.rem(shard, 2), shard // 2
     near = (node, chip * 2 + 1 - core)
     far = (node, (1 - chip) * 2 + core)
     stride = 1 << level
-    peer = (node + (1 - 2 * lax.rem(node // stride, 2)) * stride, shard)
+    other = node + (1 - 2 * lax.rem(node // stride, 2)) * stride
+    peer, cross = (other, shard), (other, far[1])
     n_blocks = raw.shape[1]
     width = normed.shape[1]
     n_chunks = own_gate.shape[0]
@@ -104,9 +126,10 @@
         copy.start()
 
     barrier = pltpu.get_barrier_semaphore()
-    for device in (near, far, peer):
+    group = (near, far, peer, cross) if direct else (near, far, peer)
+    for device in group:
         pl.semaphore_signal(barrier, inc=1, device_id=device, device_id_type=MESH)
-    pl.semaphore_wait(barrier, 3)
+    pl.semaphore_wait(barrier, len(group))
 
     n_pieces = n_blocks - 4
     per_block = BLOCK // PIECE
@@ -142,57 +165,47 @@
     both = [(kind, h) for h in range(2) for kind in range(2)]
     pieces = [(kind, i) for i in range(n_pieces) for kind in range(2)]
     pairs = ((own_gate, got_gate), (own_up, got_up), (own_down, got_down))
-    if early:
-        (passing, theirs, partial, late, their_late, scalars, their_scalars, *sems) = partner
-        slot_sems, far_sems, relay_sems, late_sems, scalar_sems = (
-            sems[i : i + 2] for i in range(0, 10, 2)
-        )
-        skipped = FIRST_LATE - 4
-        late_blocks = range(skipped, n_pieces)
-
-        def to_peer(j):
-            return remote(
-                own_piece(0, j + skipped),
-                passing.at[j],
-                slot_sems[0].at[j],
-                slot_sems[1].at[j],
-                peer,
-            )
-
-        def their_far(j):
-            return remote(
-                passing.at[j], theirs.at[0, j, head], far_sems[0].at[j], far_sems[1].at[j], far
-            )
-
-        def their_relay(j):
-            return remote(
-                theirs.at[0, j, head],
-                theirs.at[0, j, tail],
-                relay_sems[0].at[j],
-                relay_sems[1].at[j],
-                near,
-            )
-
-        def late_copy(item, j):
-            rows = pl.ds(pl.multiple_of(j * BLOCK, BLOCK), BLOCK)
-            return remote(
-                late.at[item, rows],
-                their_late.at[item, rows],
-                late_sems[0].at[item, j],
-                late_sems[1].at[item, j],
-                peer,
-            )
-
-        def early_copy(item, at=None):
-            k, c, _ = EARLY[item]
-            mine, other = partial.at[item], pairs[k][1].at[c]
-            if at is not None:
-                mine, other = mine.at[at], other.at[at]
-            return remote(mine, other, chunk_send.at[k, c], chunk_recv.at[k, c], peer)
-
-        scalar_copy = remote(
-            scalars, their_scalars, scalar_sems[0].at[0], scalar_sems[1].at[0], peer
-        )
+    first = first_late(early)
+    skipped = first - 4
+    n_late = n_pieces - skipped
+
+    def to_other(j):
+        return remote(
+            own_piece(0, j + skipped),
+            theirs.at[0, j, head] if direct else passing.at[j],
+            slot_send.at[j],
+            slot_recv.at[j],
+            cross if direct else peer,
+        )
+
+    def across(j):
+        return remote(
+            passing.at[j], theirs.at[0, j, head], across_send.at[j], across_recv.at[j], far
+        )
+
+    def pass_on(j):
+        return remote(
+            theirs.at[0, j, head], theirs.at[0, j, tail], pass_send.at[j], pass_recv.at[j], near
+        )
+
+    def late_copy(item, j):
+        rows = pl.ds(pl.multiple_of(j * BLOCK, BLOCK), BLOCK)
+        return remote(
+            late.at[item, rows],
+            their_late.at[item, rows],
+            late_send.at[item, j],
+            late_recv.at[item, j],
+            peer,
+        )
+
+    def early_copy(item, at=None):
+        k, c, _ = early[item]
+        mine, got = partial.at[item], pairs[k][1].at[c]
+        if at is not None:
+            mine, got = mine.at[at], got.at[at]
+        return remote(mine, got, chunk_send.at[k, c], chunk_recv.at[k, c], peer)
+
+    scalar_copy = remote(scalars, their_scalars, scalar_send.at[0], scalar_recv.at[0], peer)
 
     for h in range(2):
         for kind in range(2):
@@ -200,8 +213,8 @@
         for i in range(h * per_block, (h + 1) * per_block):
             for kind in range(2):
                 to_far(kind, i).start()
-            if early and i >= skipped:
-                to_peer(i - skipped).start()
+            if i >= skipped:
+                to_other(i - skipped).start()
     for copy in other_loads:
         copy.start()
     for kind, h in both:
@@ -212,8 +225,7 @@
     decay = 250.0 / (250.0 + jnp.full((8, 128), round_ref[0], jnp.int32).astype(jnp.float32))
     step = jnp.max(rate_ref[0] * decay)
     count = count_ref[0].astype(jnp.float32)
-    if early:
-        scalars[...] = rate_ref[0] * decay
+    scalars[...] = rate_ref[0] * decay
 
     def prepare(blocks, block, count):
         to = pl.ds(pl.multiple_of(block * BLOCK, BLOCK), BLOCK)
@@ -268,7 +280,7 @@
         return pl.ds(pl.multiple_of(b * part, part), part)
 
     def send_early(item):
-        k, c, blocks = EARLY[item]
+        k, c, blocks = early[item]
         weight = own_weights(c)[k]
         rows = blocks * BLOCK
 
@@ -286,13 +298,13 @@
             early_copy(item, at).start()
 
     def send_late(item, block):
-        k, c, _ = EARLY[item]
+        k, c, _ = early[item]
         at = pl.ds(pl.multiple_of(block * BLOCK, BLOCK), BLOCK)
-        to = pl.ds(pl.multiple_of((block - FIRST_LATE) * BLOCK, BLOCK), BLOCK)
+        to = pl.ds(pl.multiple_of((block - first) * BLOCK, BLOCK), BLOCK)
         late[item, to] = d_both[c, at, k * CHUNK : (k + 1) * CHUNK]
-        late_copy(item, block - FIRST_LATE).start()
-
-    ahead = 2 if early else 1
+        late_copy(item, block - first).start()
+
+    ahead = 1 + max(c for _, c, _ in early)
 
     @pl.loop(0, n_blocks)
     def _(block):
@@ -312,24 +324,24 @@
         prepare(raw, block, count)
         for c in range(ahead):
             forward(c, block)
-        if early:
-            for item, (_, _, blocks) in enumerate(EARLY):
+            items = [(item, blocks) for item, (_, chunk, blocks) in enumerate(early) if chunk == c]
+            for item, blocks in items:
                 pl.when(block >= blocks)(functools.partial(send_late, item, block))
-            for item, (_, _, blocks) in enumerate(EARLY):
+            for item, blocks in items:
                 pl.when(block == blocks - 1)(functools.partial(send_early, item))
 
-    if early:
-        scalar_copy.start()
-        for j in range(len(late_blocks)):
-            to_peer(j).wait_recv()
-            their_far(j).start()
+    scalar_copy.start()
+    if not direct:
+        for j in range(n_late):
+            to_other(j).wait_recv()
+            across(j).start()
 
     def sent(k, c, at=None):
         mine, other = (ref.at[c] if at is None else ref.at[c, at] for ref in pairs[k])
         return remote(mine, other, chunk_send.at[k, c], chunk_recv.at[k, c], peer)
 
     def if_late(k, c, act):
-        chunks = [chunk for matrix, chunk, _ in EARLY if matrix == k] if early else []
+        chunks = [chunk for matrix, chunk, _ in early if matrix == k]
         if chunks:
             pl.when(c > max(chunks))(act)
         else:
@@ -371,42 +383,39 @@
             def _(block):
                 forward(c + ahead, block)
 
-    if early:
-        for j in range(len(late_blocks)):
-            their_far(j).wait_recv()
-            their_relay(j).start()
-        for item, (_, _, blocks) in enumerate(EARLY):
-            early_copy(item).wait_recv()
-            for j in range(len(late_blocks)):
-                if FIRST_LATE + j >= blocks:
-                    late_copy(item, j).wait_recv()
-                else:
-                    their_late[item, j * BLOCK : (j + 1) * BLOCK] = jnp.zeros(
-                        (BLOCK, CHUNK), jnp.bfloat16
-                    )
-        scalar_copy.wait_recv()
-        for j in range(len(late_blocks)):
-            their_relay(j).wait_recv()
-        their_step = jnp.max(their_scalars[...])
-
-        @pl.loop(0, len(late_blocks))
-        def _(j):
-            prepare(theirs, j, None)
-
-        for item, (k, c, _) in enumerate(EARLY):
-            result = pairs[k][1].at[c]
-
-            @pl.loop(0, PARTS)
-            def _(b):
-                at = part_of(b)
-                grad = jnp.dot(
-                    normed_t[at, : len(late_blocks) * BLOCK],
-                    their_late[item],
-                    preferred_element_type=jnp.float32,
+    for j in range(n_late):
+        (to_other if direct else across)(j).wait_recv()
+        pass_on(j).start()
+    for item, (_, _, blocks) in enumerate(early):
+        early_copy(item).wait_recv()
+        for j in range(n_late):
+            if first + j >= blocks:
+                late_copy(item, j).wait_recv()
+            else:
+                their_late[item, j * BLOCK : (j + 1) * BLOCK] = jnp.zeros(
+                    (BLOCK, CHUNK), jnp.bfloat16
                 )
-                result[at] = (result[at].astype(jnp.float32) - their_step * grad).astype(
-                    jnp.bfloat16
-                )
+    scalar_copy.wait_recv()
+    for j in range(n_late):
+        pass_on(j).wait_recv()
+    their_step = jnp.max(their_scalars[...])
+
+    @pl.loop(0, n_late)
+    def _(j):
+        prepare(theirs, j, None)
+
+    for item, (k, c, _) in enumerate(early):
+        result = pairs[k][1].at[c]
+
+        @pl.loop(0, PARTS)
+        def _(b):
+            at = part_of(b)
+            grad = jnp.dot(
+                normed_t[at, : n_late * BLOCK],
+                their_late[item],
+                preferred_element_type=jnp.float32,
+            )
+            result[at] = (result[at].astype(jnp.float32) - their_step * grad).astype(jnp.bfloat16)
 
     def average(mine, theirs):
         return (0.5 * (mine.astype(jnp.float32) + theirs.astype(jnp.float32))).astype(jnp.bfloat16)
@@ -433,19 +442,19 @@
     for kind, i in pieces:
         to_far(kind, i).wait_send()
         relay(kind, i).wait_send()
-    if early:
-        scalar_copy.wait_send()
-        for j in range(len(late_blocks)):
-            to_peer(j).wait_send()
-            their_far(j).wait_send()
-            their_relay(j).wait_send()
-        for item, (_, _, blocks) in enumerate(EARLY):
-            early_copy(item).wait_send()
-            for j in range(blocks - FIRST_LATE, len(late_blocks)):
-                late_copy(item, j).wait_send()
-
-
-def one_level(level, early, count, round_index, rate, x, g, w_gate, w_up, w_down):
+    scalar_copy.wait_send()
+    for j in range(n_late):
+        to_other(j).wait_send()
+        if not direct:
+            across(j).wait_send()
+        pass_on(j).wait_send()
+    for item, (_, _, blocks) in enumerate(early):
+        early_copy(item).wait_send()
+        for j in range(blocks - first, n_late):
+            late_copy(item, j).wait_send()
+
+
+def one_level(level, shared, count, round_index, rate, x, g, w_gate, w_up, w_down):
     seq, width = x.shape
     units = w_gate.shape[1]
     n_chunks, rows = units // CHUNK, 4 * seq
@@ -457,21 +466,22 @@
     along = pltpu.VMEM((n_chunks, CHUNK, width), bf16)
     raw = pltpu.VMEM((2, rows // BLOCK, BLOCK, width), bf16)
     n_pieces = seq // PIECE
-    n_late = 4 + n_pieces - FIRST_LATE
-    late = pltpu.VMEM((len(EARLY), n_late * BLOCK, CHUNK), bf16)
+    early = EARLY_SHARED if shared else EARLY
+    n_late = 4 + n_pieces - first_late(early)
+    late = pltpu.VMEM((len(early), n_late * BLOCK, CHUNK), bf16)
     scalar = pltpu.VMEM((8, 128), jnp.float32)
     partner = [
         pltpu.VMEM((n_late, PIECE, width), bf16),
         pltpu.VMEM((1, n_late, BLOCK, width), bf16),
-        pltpu.VMEM((len(EARLY), width, CHUNK), bf16),
+        pltpu.VMEM((len(early), width, CHUNK), bf16),
         late,
         late,
         scalar,
         scalar,
     ]
-    partner += [dma((n_late,))] * 6 + [dma((len(EARLY), n_late))] * 2 + [dma((1,))] * 2
+    partner += [dma((n_late,))] * 6 + [dma((len(early), n_late))] * 2 + [dma((1,))] * 2
     mixed = pl.pallas_call(
-        functools.partial(round_kernel, level, early),
+        functools.partial(round_kernel, level, early, shared),
         out_shape=[pltpu.VMEM(w.shape, bf16) for w in (w_gate, w_up, w_down)],
         in_specs=[hbm] * 8,
         out_specs=[vmem] * 3,
@@ -503,7 +513,7 @@
             dma((2, n_pieces)),
             dma((3, n_chunks)),
             dma((3, n_chunks)),
-            *(partner if early else ()),
+            *partner,
         ],
         compiler_params=pltpu.CompilerParams(
             collective_id=level, has_side_effects=True, vmem_limit_bytes=44 << 20
@@ -545,7 +555,7 @@
     levels = lax.axis_size("node").bit_length() - 1
     mixed = lax.switch(
         lax.rem(round_index[0], levels),
-        [functools.partial(one_level, level, level < levels - 1) for level in range(levels)],
+        [functools.partial(one_level, level, level == levels - 1) for level in range(levels)],
         counts,
         round_index,
         rates,

time: 201 us -> 201 us (level)
  no operation moved by 1% of the time
where the time goes in v6:
time: 201 us
  Pallas kernels  199 us (99%)
    pallas_call x1, Pallas kernels, one_level(): pl.pallas_call(functools.partial(round_kernel, level, early, shared), out...  196 us

profile of v6, /device:TPU:1, one launch (start us, length us, event | category | flops | bytes accessed | tf_op | source)
XLA Modules:
  0.0 201.1 jit_solution(10761426211437590501)
XLA Ops:
  1.3 199.6 %conditional.1 = ((bf16[1152,1152]{1,0:T(8,128)(2,1)}, bf16[1152,1152]{1,0:T(8,128)(2,1)}, bf16[1152,1152]{1,0:T(8,128)(2,1)})) conditional(s32[]{:T(128)} %bitcast, (s32[1]{0:T(128)}, s32[1]{0:T(128)}, f32[1]{0:T(128)}, bf16[256,1152]{1,0:T(8,128)(2,1)}, bf16[256,1152]{1,0:T(8,128)(2,1)}, ...), branch_computations={%region_0.0_spmd.clone, %region_1.0_spmd.clone, %region_2.0_spmd.c... | conditional | flops 16307453952 | bytes 17104904 | solution.py:556
  1.5 195.9 %round_level_3.1 = (bf16[1152,1152]{1,0:T(8,128)(2,1)S(1)}, bf16[1152,1152]{1,0:T(8,128)(2,1)S(1)}, bf16[1152,1152]{1,0:T(8,128)(2,1)S(1)}) custom-call(s32[1]{0:T(128)} %get-tuple-element.212.count_hbm, s32[1]{0:T(128)} %get-tuple-element.213.round_hbm, f32[1]{0:T(128)} %get-tuple-element.214.rate_hbm, bf16[256,1152]{1,0:T(8,128)(2,1)} %get-tuple-element.215.x_hbm, ...), custom_call_target="tpu_custom_call" | custom-call | flops 16307453952 | bytes 17104896 | tf_op jit(solution)/shard_map/cond/branch_3_fun/round_level_3/pallas_call | solution.py:483
  197.4 3.3 %write_out.8 = (bf16[1152,1152]{1,0:T(8,128)(2,1)}, bf16[1152,1152]{1,0:T(8,128)(2,1)}, bf16[1152,1152]{1,0:T(8,128)(2,1)}) custom-call(bf16[1152,1152]{1,0:T(8,128)(2,1)S(1)} %get-tuple-element.220.gate, bf16[1152,1152]{1,0:T(8,128)(2,1)S(1)} %get-tuple-element.221.up, bf16[1152,1152]{1,0:T(8,128)(2,1)S(1)} %get-tuple-element.222.down), custom_call_target="tpu_custom_call" | custom-call | tf_op jit(solution)/shard_map/cond/branch_3_fun/write_out/pallas_call | solution.py:543

commit v7 on v6

--- a/solution.py
+++ b/solution.py
@@ -284,9 +284,9 @@
         weight = own_weights(c)[k]
         rows = blocks * BLOCK
 
-        @pl.loop(0, PARTS)
+        @pl.loop(0, width // BLOCK)
         def _(b):
-            at = part_of(b)
+            at = pl.ds(pl.multiple_of(b * BLOCK, BLOCK), BLOCK)
             grad = jnp.dot(
                 normed_t[at, :rows],
                 d_both[c, :rows, k * CHUNK : (k + 1) * CHUNK],
@@ -420,23 +420,6 @@
     def average(mine, theirs):
         return (0.5 * (mine.astype(jnp.float32) + theirs.astype(jnp.float32))).astype(jnp.bfloat16)
 
-    @pl.loop(0, n_chunks)
-    def _(c):
-        units = units_of(c)
-
-        if_late(0, c, lambda: sent(0, c).wait_recv())
-        mixed_gate[:, units] = average(own_gate[c], got_gate[c])
-        if_late(1, c, lambda: sent(1, c).wait_recv())
-        mixed_up[:, units] = average(own_up[c], got_up[c])
-        sent(2, c).wait_recv()
-        mixed_down[units] = average(own_down[c], got_down[c])
-
-    @pl.loop(0, n_chunks)
-    def _(c):
-        if_late(0, c, lambda: sent(0, c).wait_send())
-        if_late(1, c, lambda: sent(1, c).wait_send())
-        sent(2, c).wait_send()
-
     for kind, h in both:
         to_near(kind, h).wait_send()
     for kind, i in pieces:
@@ -452,6 +435,26 @@
         early_copy(item).wait_send()
         for j in range(blocks - first, n_late):
             late_copy(item, j).wait_send()
+
+    @pl.loop(0, n_chunks)
+    def _(c):
+        units = units_of(c)
+
+        if_late(0, c, lambda: sent(0, c).wait_recv())
+        mixed_gate[:, units] = average(own_gate[c], got_gate[c])
+        if_late(1, c, lambda: sent(1, c).wait_recv())
+        mixed_up[:, units] = average(own_up[c], got_up[c])
+        sent(2, c).wait_recv()
+        mixed_down[units] = average(own_down[c], got_down[c])
+
+        @pl.when(c < n_chunks - 1)
+        def _():
+            if_late(0, c, lambda: sent(0, c).wait_send())
+            if_late(1, c, lambda: sent(1, c).wait_send())
+            sent(2, c).wait_send()
+
+    for k in range(3):
+        sent(k, n_chunks - 1).wait_send()
 
 
 def one_level(level, shared, count, round_index, rate, x, g, w_gate, w_up, w_down):

time: 201 us -> 201 us (level)
  no operation moved by 1% of the time
where the time goes in v7:
time: 201 us
  Pallas kernels  199 us (99%)
    pallas_call x1, Pallas kernels, one_level(): pl.pallas_call(functools.partial(round_kernel, level, early, shared), out...  196 us

profile of v7, /device:TPU:1, one launch (start us, length us, event | category | flops | bytes accessed | tf_op | source)
XLA Modules:
  0.0 200.9 jit_solution(5290914162149117800)
XLA Ops:
  1.3 199.4 %conditional.1 = ((bf16[1152,1152]{1,0:T(8,128)(2,1)}, bf16[1152,1152]{1,0:T(8,128)(2,1)}, bf16[1152,1152]{1,0:T(8,128)(2,1)})) conditional(s32[]{:T(128)} %bitcast, (s32[1]{0:T(128)}, s32[1]{0:T(128)}, f32[1]{0:T(128)}, bf16[256,1152]{1,0:T(8,128)(2,1)}, bf16[256,1152]{1,0:T(8,128)(2,1)}, ...), branch_computations={%region_0.0_spmd.clone, %region_1.0_spmd.clone, %region_2.0_spmd.c... | conditional | flops 16307453952 | bytes 17104904 | solution.py:559
  1.5 195.7 %round_level_3.1 = (bf16[1152,1152]{1,0:T(8,128)(2,1)S(1)}, bf16[1152,1152]{1,0:T(8,128)(2,1)S(1)}, bf16[1152,1152]{1,0:T(8,128)(2,1)S(1)}) custom-call(s32[1]{0:T(128)} %get-tuple-element.212.count_hbm, s32[1]{0:T(128)} %get-tuple-element.213.round_hbm, f32[1]{0:T(128)} %get-tuple-element.214.rate_hbm, bf16[256,1152]{1,0:T(8,128)(2,1)} %get-tuple-element.215.x_hbm, ...), custom_call_target="tpu_custom_call" | custom-call | flops 16307453952 | bytes 17104896 | tf_op jit(solution)/shard_map/cond/branch_3_fun/round_level_3/pallas_call | solution.py:486
  197.2 3.3 %write_out.8 = (bf16[1152,1152]{1,0:T(8,128)(2,1)}, bf16[1152,1152]{1,0:T(8,128)(2,1)}, bf16[1152,1152]{1,0:T(8,128)(2,1)}) custom-call(bf16[1152,1152]{1,0:T(8,128)(2,1)S(1)} %get-tuple-element.220.gate, bf16[1152,1152]{1,0:T(8,128)(2,1)S(1)} %get-tuple-element.221.up, bf16[1152,1152]{1,0:T(8,128)(2,1)S(1)} %get-tuple-element.222.down), custom_call_target="tpu_custom_call" | custom-call | tf_op jit(solution)/shard_map/cond/branch_3_fun/write_out/pallas_call | solution.py:546
